TPU v7x, 512 devices: a whole 4x8x8 slice. The times are simulated.
512 devices in a mesh: row: 32 (over x, y), shift: 16 (over z, core).
Axes of the slice: x: 4, y: 8, z: 8, core: 2. Of those that a mesh axis runs over, the one named last changes fastest.
Arguments:
- snapshots: bfloat16 [4096, 2, 128], P('row'), may hold values from -6 to 6
- tail_sensors: bfloat16 [128, 2, 128], replicated, may hold values from -6 to 6
- shift_offsets: int32 [48], P('shift'), may hold values from 0 to 128
- start_basis: float32 [64, 4096], P(None, 'row'), may hold values from -0.09375 to 0.09375
Outputs:
- covariance: float32 [4096, 4096], P('row', 'shift')
- signal_basis: float32 [64, 4096], P(None, 'row')
Inputs may be any that keep to these rules, and one draw needn't show every extreme that they name: `shift_offsets`: each shift's first sensor.
All inputs are finite; a program needn't handle non-finite values.
Results may differ from a plain program's by a relative error of at most 0.0031.
Values may be sent and summed in bfloat16 or wider, within the bound.
A program may use at most 64 MiB of HBM per device.

v0:
```python
import jax
import jax.numpy as jnp
from jax import lax
from jax.sharding import Mesh
from jax.sharding import PartitionSpec as P

M = 4096
SNAPS = 128
ITERS = 2
ROW = ("row_0", "row_1")


half_root = 0.7071067811865476


def joined_along(tiles, dim):
    tiles = jnp.moveaxis(tiles, 0, dim)
    lengths = tiles.shape
    return tiles.reshape(*lengths[:dim], lengths[dim] * lengths[dim + 1], *lengths[dim + 2 :])


def stacked_from(x, axes, order):
    tiles = x
    for k in order:
        tiles = lax.all_gather(tiles, axes[k])
    done = order[::-1]
    back = [done.index(k) for k in range(len(axes))]
    tiles = tiles.transpose(*back, *range(len(axes), tiles.ndim))
    return tiles.reshape(-1, *x.shape)


def whole_of(x, axes, order, dim):
    return joined_along(stacked_from(x, axes, order), dim)


def sent_to_all(x, axis):
    copies = jnp.broadcast_to(x, (lax.axis_size(axis), *x.shape))
    return lax.all_to_all(copies, axis, split_axis=0, concat_axis=0, tiled=True)


def gather_directly(x, axis, dim):
    tiles = sent_to_all(x, axis)
    return joined_along(tiles, dim)


def total_of_pieces(x, axis):
    tiles = lax.all_gather(x, axis)
    return tiles.sum(axis=0)


def make_some(extended, offset, start, count):
    window = lax.dynamic_slice_in_dim(extended, offset + start, count, 0).astype(jnp.float32)
    mirror = lax.dynamic_slice_in_dim(extended, offset + M - start - count, count, 0).astype(
        jnp.float32
    )[::-1]
    summed_pair = window + mirror
    difference = window - mirror
    upper_rows = jnp.concatenate([summed_pair[:, 0], summed_pair[:, 1]], axis=1)
    bottom = jnp.concatenate([difference[:, 1], -difference[:, 0]], axis=1)
    positions = start + jnp.arange(count, dtype=jnp.int32)
    chosen = jnp.where((positions < M // 2)[:, None], upper_rows, bottom)
    return (chosen * half_root).astype(jnp.bfloat16)


def factor(gram_matrix):
    lower_factor = jnp.linalg.cholesky(gram_matrix)
    identity = jnp.eye(gram_matrix.shape[0], dtype=jnp.float32)
    return jax.scipy.linalg.solve_triangular(lower_factor, identity, lower=True)


def per_device(snapshots, tail_sensors, shift_offsets, start_basis):
    block_rows = snapshots.shape[0]
    row_index = lax.axis_index(ROW)
    shift_index = lax.axis_index("shift")
    col_count = M // lax.axis_size("shift")
    normalizer = 1.0 / (SNAPS * shift_offsets.shape[0] * lax.axis_size("shift"))
    gathered = whole_of(snapshots, ROW, (0, 1), 0)
    extended = jnp.concatenate([gathered, tail_sensors], 0)
    every_offset = gather_directly(shift_offsets, "shift", 0)
    row_start = row_index * block_rows
    col_start = shift_index * col_count

    def add_block(which, running):
        offset = every_offset[which]
        own_rows = make_some(extended, offset, row_start, block_rows)
        col_rows = make_some(extended, offset, col_start, col_count)
        return running + lax.dot_general(
            own_rows, col_rows, (((1,), (1,)), ((), ())), preferred_element_type=jnp.float32
        )

    summed_block = lax.fori_loop(
        0, every_offset.shape[0], add_block, jnp.zeros((block_rows, col_count), jnp.float32)
    )
    cov_out = summed_block * normalizer
    basis_rows = gather_directly(start_basis, ROW, 1)
    own_basis = start_basis
    for sweep in range(ITERS):
        basis_cols = lax.dynamic_slice_in_dim(basis_rows, shift_index * col_count, col_count, 1)
        column_terms = lax.dot_general(
            basis_cols, cov_out, (((1,), (1,)), ((), ())), precision=lax.Precision.HIGHEST
        )
        mapped = total_of_pieces(column_terms, "shift")
        full_image = gather_directly(mapped, ROW, 1)
        gram_matrix = jnp.dot(full_image, full_image.T, precision=lax.Precision.HIGHEST)
        basis_rows = jnp.dot(factor(gram_matrix), full_image, precision=lax.Precision.HIGHEST)
        own_basis = lax.dynamic_slice_in_dim(basis_rows, row_index * block_rows, block_rows, 1)
    return (cov_out, own_basis)


def solution(mesh):
    split = Mesh(mesh.devices.reshape(4, 8, mesh.shape["shift"]), ("row_0", "row_1", "shift"))
    in_specs = (P(ROW, None, None), P(), P("shift"), P(None, ROW))
    out_specs = (P(ROW, "shift"), P(None, ROW))
    return jax.shard_map(
        per_device, mesh=split, in_specs=in_specs, out_specs=out_specs, check_vma=False
    )
```

profile of v0, /device:TPU:1, one launch (start us, length us, event | category | flops | bytes accessed | tf_op | source)
XLA Modules:
  0.0 395.8 jit_solution(15527877105455967366)
XLA Ops:
  7.2 0.9 copy.63
  8.1 11.3 %all-gather = bf16[512,2,128]{2,0,1:T(8,128)(2,1)} all-gather(bf16[128,2,128]{2,0,1:T(8,128)(2,1)S(1)} %copy.63), channel_id=2, replica_groups=mesh['row_0'=4,'row_1'=8,'shift'=16] {'row_0'}, dimensions={0}, use_global_device_ids=true | all-gather | bytes 327680 | tf_op jit(solution)/shard_map/all_gather | solution.py:25
  20.0 20.7 %all_to_all.21 = s32[16,1,3]{2,1,0:T(1,128)S(1)} all-to-all(s32[16,1,3]{2,1,0:T(1,128)S(1)} %broadcast_in_dim.73), channel_id=1, replica_groups=mesh['row_0'=4,'row_1'=8,'shift'=16] {'shift'}, dimensions={0} | all-to-all | bytes 384 | tf_op jit(solution)/shard_map/all_to_all | solution.py:38
  40.8 1.9 broadcast_in_dim.74
  42.6 9.3 %all-to-all-start.1 = ((f32[32,64,128]{2,1,0:T(8,128)}), f32[32,64,128]{2,1,0:T(8,128)S(1)}, u32[]{:S(2)}, u32[]{:S(2)}) async-start(f32[32,64,128]{2,1,0:T(8,128)} %broadcast_in_dim.74), calls=%async_computation.1 | async-start | bytes 2097152 | tf_op jit(solution)/shard_map/all_to_all | solution.py:38
  53.3 33.4 %all-to-all-done.1 = f32[32,64,128]{2,1,0:T(8,128)S(1)} async-done(((f32[32,64,128]{2,1,0:T(8,128)}), f32[32,64,128]{2,1,0:T(8,128)S(1)}, u32[]{:S(2)}, u32[]{:S(2)}) %all-to-all-start.1) | async-done | bytes 1048608 | tf_op jit(solution)/shard_map/all_to_all | solution.py:38
  86.6 1.1 copy_bitcast_fusion
  87.7 1.7 copy.65
  89.6 162.9 %while.18 = (s32[]{:T(128)}, f32[128,256]{1,0:T(8,128)S(1)}, s32[]{:T(128)}, s32[48]{0:T(128)S(1)}, bf16[4224,2,128]{2,0,1:T(8,128)(2,1)S(1)}, /*index=5*/s32[]{...) while((s32[]{:T(128)}, f32[128,256]{1,0:T(8,128)S(1)}, ...), condition=%wide.region_1.2_spmd.clone, body=%wide.region_0.1_spmd.clone.sunk | while | flops 17777428 | bytes 5375111 | solution.py:91
  252.5 1.2 fusion.24
  253.7 21.2 %all-gather.2 = f32[1024,128]{1,0:T(8,128)S(1)} all-gather(f32[64,128]{1,0:T(8,128)S(1)} %fusion.24), channel_id=4, replica_groups=mesh['row_0'=4,'row_1'=8,'shift'=16] {'shift'}, dimensions={0}, use_global_device_ids=true | all-gather | bytes 557056 | tf_op jit(solution)/shard_map/all_gather | solution.py:47
  275.0 33.0 %all_to_all.22 = f32[32,64,128]{2,1,0:T(8,128)S(1)} all-to-all(f32[32,64,128]{2,1,0:T(8,128)S(1)} %broadcast_in_dim.75), channel_id=1, replica_groups=mesh['row_0'=4,'row_1'=8,'shift'=16] {'row_0','row_1'}, dimensions={0} | all-to-all | bytes 2097152 | tf_op jit(solution)/shard_map/all_to_all | solution.py:38
  308.0 1.0 convolution_bitcast_fusion.1
  309.1 5.8 %cholesky.44 = f32[64,64]{1,0:T(8,128)S(1)} custom-call(f32[64,64]{1,0:T(8,128)S(1)} %fusion.35), custom_call_target="Cholesky" | custom-call | tf_op jit(solution)/shard_map/jit(cholesky)/cholesky | solution.py:66
  316.3 4.9 %custom-call.7 = f32[1,64,64]{1,2,0:T(8,128)S(1)} custom-call(f32[1,64,64]{2,1,0:T(8,128)S(1)} %fusion.30), custom_call_target="InvertDiagBlocksLowerTriangular" | custom-call | tf_op jit(solution)/shard_map/jit(_solve_triangular)/triangular_solve | solution.py:68
  321.4 1.0 fusion.17
  322.7 19.9 %all-gather.3 = f32[1024,128]{1,0:T(8,128)S(1)} all-gather(f32[64,128]{1,0:T(8,128)S(1)} %fusion.22), channel_id=5, replica_groups=mesh['row_0'=4,'row_1'=8,'shift'=16] {'shift'}, dimensions={0}, use_global_device_ids=true | all-gather | bytes 557056 | tf_op jit(solution)/shard_map/all_gather | solution.py:47
  342.7 1.1 broadcast_in_dim.76
  343.8 4.8 %all-to-all-start.3 = ((f32[32,64,128]{2,1,0:T(8,128)}), f32[32,64,128]{2,1,0:T(8,128)S(1)}, u32[]{:S(2)}, u32[]{:S(2)}) async-start(f32[32,64,128]{2,1,0:T(8,128)} %broadcast_in_dim.76), calls=%async_computation.3 | async-start | bytes 2097152 | tf_op jit(solution)/shard_map/all_to_all | solution.py:38
  348.6 25.3 %all-to-all-done.3 = f32[32,64,128]{2,1,0:T(8,128)S(1)} async-done(((f32[32,64,128]{2,1,0:T(8,128)}), f32[32,64,128]{2,1,0:T(8,128)S(1)}, u32[]{:S(2)}, u32[]{:S(2)}) %all-to-all-start.3) | async-done | bytes 1048608 | tf_op jit(solution)/shard_map/all_to_all | solution.py:38
  373.9 1.0 convolution_bitcast_fusion
  374.9 5.8 %cholesky.55 = f32[64,64]{1,0:T(8,128)S(1)} custom-call(f32[64,64]{1,0:T(8,128)S(1)} %fusion.33), custom_call_target="Cholesky" | custom-call | tf_op jit(solution)/shard_map/jit(cholesky)/cholesky | solution.py:66
  382.1 4.9 %custom-call.8 = f32[1,64,64]{1,2,0:T(8,128)S(1)} custom-call(f32[1,64,64]{2,1,0:T(8,128)S(1)} %fusion.31), custom_call_target="InvertDiagBlocksLowerTriangular" | custom-call | tf_op jit(solution)/shard_map/jit(_solve_triangular)/triangular_solve | solution.py:68
  387.3 1.0 fusion.14
  (608 shorter events, 69.9 us)
Async XLA Ops:
  7.2 44.8 %copy-start.1 = (bf16[128,2,128]{2,1,0:T(2,128)(2,1)S(1)}, bf16[128,2,128]{2,1,0:T(2,128)(2,1)}, u32[]{:S(2)}) copy-start(bf16[128,2,128]{2,1,0:T(2,128)(2,1)} %param.10) | copy-start | bytes 196612
  7.2 80.5 %all-gather.6.cloned.1.call-start = ((), (), s32[]{:S(2)}) async-start(), calls=%async_computation.4 | async-start | bytes 2359296 | tf_op jit(solution)/shard_map/all_gather | solution.py:25
  42.6 44.0 %all-to-all-start.1 = ((f32[32,64,128]{2,1,0:T(8,128)}), f32[32,64,128]{2,1,0:T(8,128)S(1)}, u32[]{:S(2)}, u32[]{:S(2)}) async-start(f32[32,64,128]{2,1,0:T(8,128)} %broadcast_in_dim.74), calls=%async_computation.1 | async-start | bytes 2097152 | tf_op jit(solution)/shard_map/all_to_all | solution.py:38
  252.5 70.0 %copy-start = (f32[128,256]{1,0:T(8,128)}, f32[128,256]{1,0:T(8,128)S(1)}, u32[]{:S(2)}) copy-start(f32[128,256]{1,0:T(8,128)S(1)} %broadcast_multiply_fusion) | copy-start | bytes 393220
  343.8 30.1 %all-to-all-start.3 = ((f32[32,64,128]{2,1,0:T(8,128)}), f32[32,64,128]{2,1,0:T(8,128)S(1)}, u32[]{:S(2)}, u32[]{:S(2)}) async-start(f32[32,64,128]{2,1,0:T(8,128)} %broadcast_in_dim.76), calls=%async_computation.3 | async-start | bytes 2097152 | tf_op jit(solution)/shard_map/all_to_all | solution.py:38
Sparse Core Ops, SparseCore 0:
  19.5 65.2 all-gather.5
where the time goes:
time: 400 us; the launch traced here: 396 us
  blocking collectives  106 us (26%)
  loops' own time  99.6 us (25%)
  waiting for transfers between devices  58.6 us (15%)
  local copies, waits for them, and re-layouts  47.8 us (12%)
  other arithmetic  35.5 us (9%)
  matrix products  19.8 us (5%)
  between operations  14.3 us (4%)
  starting transfers between devices  14.1 us (4%)
    another operation x1, loops' own time, per_device(): lax.fori_loop(0, every_offset.shape[0], add_block, jnp.zeros((block_rows,...  99.6 us
    all_to_all x2, waiting for transfers between devices, sent_to_all(): return lax.all_to_all(copies, axis, split_axis=0, concat_axis=0, tiled=True)  58.6 us
    all_to_all x2, blocking collectives, sent_to_all(): return lax.all_to_all(copies, axis, split_axis=0, concat_axis=0, tiled=True)  53.7 us
    all_gather x2, blocking collectives, total_of_pieces(): tiles = lax.all_gather(x, axis)  41.1 us
    dynamic_slice x48, local copies, waits for them, and re-layouts, add_block(): offset = every_offset[which]  28.3 us
    all_to_all x2, starting transfers between devices, sent_to_all(): return lax.all_to_all(copies, axis, split_axis=0, concat_axis=0, tiled=True)  14.1 us
    dot_general x48, matrix products, add_block(): lax.dot_general(own_rows, col_rows, (((1,), (1,)), ((), ())), preferred_e...  13.9 us
    another operation x6, other arithmetic, factor(): lower_factor = jnp.linalg.cholesky(gram_matrix)  13 us
  transfers between devices with their start and end apart: 3, of which 2 were waited for; matrix products, arithmetic and copies ran while one was open for 1% of the time, Pallas kernels for 0%

commit v1 on v0

v1 whole, which is shorter than its diff:
```python
import jax
import jax.numpy as jnp
from jax import lax
from jax.experimental import pallas as pl
from jax.experimental.pallas import tpu as pltpu
from jax.sharding import PartitionSpec as P

M = 4096
K = 64
SNAPS = 128
SHIFTS = 48
ROWS = 32
COLS = 16
BLOCK = 128
HALF_ROOT = 0.7071067811865476
MESH = pl.DeviceIdType.MESH
HIGHEST = lax.Precision.HIGHEST
F32 = jnp.float32
BF16 = jnp.bfloat16


def signal_peers(barrier, r, t):
    def plane(k, _):
        pl.semaphore_signal(
            barrier, inc=1, device_id={"row": lax.rem(r + k, ROWS)}, device_id_type=MESH
        )
        return _

    def line(k, _):
        pl.semaphore_signal(
            barrier, inc=1, device_id={"shift": lax.rem(t + k, COLS)}, device_id_type=MESH
        )
        return _

    lax.fori_loop(1, ROWS, plane, 0)
    lax.fori_loop(1, COLS, line, 0)


def gather_kernel(own_ref, tail_ref, offs_ref, got_ref, offs_out, send_sem, near_sem, recv_sem, offs_send, offs_recv):
    r = lax.axis_index("row")
    t = lax.axis_index("shift")
    barrier = pltpu.get_barrier_semaphore()
    signal_peers(barrier, r, t)
    pl.semaphore_wait(barrier, ROWS - 1 + COLS - 1)

    def block_copy(slot, dest, send):
        return pltpu.make_async_remote_copy(
            src_ref=own_ref,
            dst_ref=got_ref.at[slot],
            send_sem=send,
            recv_sem=recv_sem.at[slot],
            device_id={"row": dest},
            device_id_type=MESH,
        )

    firsts = (2 * t, 30 - 2 * t)
    for group, first in enumerate(firsts):
        place = r - first

        @pl.when((place >= 0) & (place <= 2))
        def _():
            slot = 3 + 3 * group + place

            def send(k, c):
                block_copy(slot, lax.rem(r + k, ROWS), send_sem.at[group, k]).start()
                return c

            lax.fori_loop(1, ROWS, send, 0)
            got_ref[slot] = own_ref[...]

    @pl.when(r >= 1)
    def _():
        block_copy(0, r - 1, near_sem.at[0]).start()

    block_copy(1, 31 - r, near_sem.at[1]).start()

    @pl.when((r >= 1) & (r != 16))
    def _():
        block_copy(2, 32 - r, near_sem.at[2]).start()

    def offs_copy(k):
        return pltpu.make_async_remote_copy(
            src_ref=offs_ref,
            dst_ref=offs_out.at[t],
            send_sem=offs_send,
            recv_sem=offs_recv,
            device_id={"shift": lax.rem(t + k, COLS)},
            device_id_type=MESH,
        )

    def send_offs(k, c):
        offs_copy(k).start()
        return c

    lax.fori_loop(1, COLS, send_offs, 0)
    offs_out[t] = offs_ref[...]

    @pl.when(r == 31)
    def _():
        got_ref[0] = tail_ref[...]

    @pl.when(r == 0)
    def _():
        got_ref[2] = tail_ref[...]

    @pl.when(r == 16)
    def _():
        got_ref[2] = own_ref[...]

    @pl.when(t == 15)
    def _():
        got_ref[5] = tail_ref[...]

    @pl.when(t == 0)
    def _():
        got_ref[8] = tail_ref[...]

    def arrived(slot):
        block_copy(slot, r, near_sem.at[0]).wait_recv()

    @pl.when(r != 31)
    def _():
        arrived(0)

    arrived(1)

    @pl.when((r != 0) & (r != 16))
    def _():
        arrived(2)

    for group, first in enumerate(firsts):
        for place in range(3):
            block = first + place

            @pl.when((block != r) & (block != 32))
            def _():
                arrived(3 + 3 * group + place)

    every = offs_out.at[pl.ds(0, COLS - 1)]
    whole = pltpu.make_async_remote_copy(
        src_ref=every,
        dst_ref=every,
        send_sem=offs_send,
        recv_sem=offs_recv,
        device_id={"shift": t},
        device_id_type=MESH,
    )
    whole.wait_recv()
    whole.wait_send()

    for group, first in enumerate(firsts):
        place = r - first

        @pl.when((place >= 0) & (place <= 2))
        def _():
            def done(k, c):
                block_copy(3, r, send_sem.at[group, k]).wait_send()
                return c

            lax.fori_loop(1, ROWS, done, 0)

    @pl.when(r >= 1)
    def _():
        block_copy(0, r, near_sem.at[0]).wait_send()

    block_copy(1, r, near_sem.at[1]).wait_send()

    @pl.when((r >= 1) & (r != 16))
    def _():
        block_copy(2, r, near_sem.at[2]).wait_send()


def lower_inverse(gram):
    lanes = lax.broadcasted_iota(jnp.int32, (8, 128), 1)
    subs = lax.broadcasted_iota(jnp.int32, (8, 128), 0)
    rows = [gram[8 * i : 8 * i + 8] + jnp.where(lanes == subs + 8 * i, 1.0, 0.0) for i in range(8)]
    out = []
    for b in range(8):
        cols = [
            {i: jnp.broadcast_to(rows[i][:, 64 + 8 * b + j : 65 + 8 * b + j], (8, 128)) for i in range(b, 8)}
            for j in range(8)
        ]
        scale = jnp.zeros((8, 128), F32)
        for j in range(8):
            pivot = jnp.broadcast_to(cols[j][b][j : j + 1], (8, 128))
            root = lax.rsqrt(pivot)
            inverse = root * root
            scale = jnp.where(subs == j, root, scale)
            lead = jnp.broadcast_to(rows[b][j : j + 1], (8, 128))
            heads = {l: jnp.broadcast_to(cols[l][b][j : j + 1], (8, 128)) for l in range(j + 1, 8)}
            for i in range(b, 8):
                factor = cols[j][i] * inverse
                if i == b:
                    factor = jnp.where(subs > j, factor, 0.0)
                rows[i] = rows[i] - factor * lead
                for l in range(j + 1, 8):
                    cols[l][i] = cols[l][i] - factor * heads[l]
        out.append(rows[b] * scale)
    return jnp.concatenate(out, 0)[:, :64]


def padded_gram(x):
    both = jnp.concatenate([jnp.zeros_like(x), x], 0)
    return lax.dot_general(x, both, (((1,), (1,)), ((), ())), precision=HIGHEST, preferred_element_type=F32)


def music_kernel(
    own_ref, got_ref, offs_ref, start_ref, cov_ref, basis_ref,
    row_w, row_m, col_w, col_m, acc,
    part1, land1, map1, part2, land2, sum2, part3, land3, sum3,
    send_sem, recv_sem,
):
    r = lax.axis_index("row")
    t = lax.axis_index("shift")
    barrier = pltpu.get_barrier_semaphore()
    signal_peers(barrier, r, t)

    up = lax.broadcasted_iota(jnp.int32, (BLOCK, BLOCK), 0)
    across = lax.broadcasted_iota(jnp.int32, (BLOCK, BLOCK), 1)
    flip = jnp.where(up + across == BLOCK - 1, 1.0, 0.0).astype(BF16)

    def put(window, place, block, top):
        re, im = block[0].astype(F32) * HALF_ROOT, block[1].astype(F32) * HALF_ROOT
        window[0, pl.ds(place * BLOCK, BLOCK), :] = jnp.where(top, re, im)
        window[1, pl.ds(place * BLOCK, BLOCK), :] = jnp.where(top, im, -re)

    def put_flipped(mirror, place, block, top):
        re = jnp.dot(flip, block[0], preferred_element_type=F32) * HALF_ROOT
        im = jnp.dot(flip, block[1], preferred_element_type=F32) * HALF_ROOT
        mirror[0, pl.ds(place * BLOCK, BLOCK), :] = jnp.where(top, re, -im)
        mirror[1, pl.ds(place * BLOCK, BLOCK), :] = jnp.where(top, im, re)

    row_top, col_top = r < ROWS // 2, t < COLS // 2
    put(row_w, 0, own_ref[...], row_top)
    put(row_w, 1, got_ref[0], row_top)
    put_flipped(row_m, 0, got_ref[2], row_top)
    put_flipped(row_m, 1, got_ref[1], row_top)
    for place in range(3):
        put(col_w, place, got_ref[3 + place], col_top)
        put_flipped(col_m, place, got_ref[8 - place], col_top)

    def pairs(window, mirror, offset, count):
        parts = []
        for c in range(2):
            a = window[c, pl.ds(offset, count), :]
            b = mirror[c, pl.ds(BLOCK - offset, count), :]
            parts.append((a + b).astype(BF16))
        return parts

    acc[...] = jnp.zeros_like(acc)

    def some(i, c):
        lhs, rhs = [], []
        for j in range(3):
            offset = offs_ref[i, 0, j]
            lhs += pairs(row_w, row_m, offset, BLOCK)
            rhs += pairs(col_w, col_m, offset, 2 * BLOCK)
        acc[...] += lax.dot_general(
            jnp.concatenate(lhs, 1), jnp.concatenate(rhs, 1), (((1,), (1,)), ((), ())), preferred_element_type=F32
        )
        return c

    lax.fori_loop(0, COLS, some, 0)
    cov = acc[...] * (1.0 / (SNAPS * SHIFTS))
    cov_ref[...] = cov

    first = jnp.dot(start_ref[...], cov, precision=HIGHEST, preferred_element_type=F32)
    for c in range(2):
        for a in range(8):
            part1[8 * c + a] = first[8 * a : 8 * a + 8, BLOCK * c : BLOCK * c + BLOCK]

    pl.semaphore_wait(barrier, ROWS - 1 + COLS - 1)

    def copy(src, dst, phase, where):
        return pltpu.make_async_remote_copy(
            src_ref=src,
            dst_ref=dst,
            send_sem=send_sem.at[phase],
            recv_sem=recv_sem.at[phase],
            device_id=where,
            device_id_type=MESH,
        )

    def over(count, body):
        def step(k, c):
            body(k)
            return c

        lax.fori_loop(1, count, step, 0)

    def total(phase, buffer, count):
        every = buffer.at[pl.ds(0, count)]
        return copy(every, every, phase, {"row": r})

    def scatter1(k):
        dest = lax.rem(r + k, ROWS)
        copy(part1.at[dest // 2], land1.at[r], 0, {"row": dest}).start()

    over(ROWS, scatter1)
    land1[r] = part1[r // 2]
    total(0, land1, ROWS - 1).wait_recv()
    mine = r // 2
    map1[mine] = jnp.sum(land1[...], axis=0)

    def spread1(k):
        copy(map1.at[mine], map1.at[mine], 1, {"row": lax.rem(r + 2 * k, ROWS)}).start()

    over(ROWS // 2, spread1)
    total(1, map1, ROWS // 2 - 1).wait_recv()
    mapped = jnp.concatenate([map1[0:8].reshape(K, BLOCK), map1[8:16].reshape(K, BLOCK)], 1)

    gram1 = padded_gram(mapped)
    second = lax.dot_general(
        mapped, cov_ref[...], (((1,), (1,)), ((), ())), precision=HIGHEST, preferred_element_type=F32
    )
    for a in range(8):
        part2[a] = second[8 * a : 8 * a + 8]
        part2[8 + a] = gram1[8 * a : 8 * a + 8]

    def scatter2(k):
        dest = lax.rem(t + k, COLS)
        copy(part2.at[dest], land2.at[t], 2, {"shift": dest}).start()

    over(COLS, scatter2)
    land2[t] = part2[t]
    total(2, land2, COLS - 1).wait_recv()
    sum2[t] = jnp.sum(land2[...], axis=0)

    def spread2(k):
        copy(sum2.at[t], sum2.at[t], 3, {"shift": lax.rem(t + k, COLS)}).start()

    over(COLS, spread2)
    total(3, sum2, COLS - 1).wait_recv()
    factor1 = lower_inverse(sum2[8:16].reshape(K, BLOCK))
    mapped2 = jnp.dot(factor1, sum2[0:8].reshape(K, BLOCK), precision=HIGHEST, preferred_element_type=F32)
    gram2 = padded_gram(mapped2)
    for a in range(16):
        part3[a] = gram2[4 * a : 4 * a + 4]

    def spread3(k):
        copy(part3.at[t], land3.at[r], 4, {"row": lax.rem(r + k, ROWS)}).start()

    over(ROWS, spread3)
    land3[r] = part3[t]
    total(4, land3, ROWS - 1).wait_recv()
    sum3[t] = jnp.sum(land3[...], axis=0)

    def spread4(k):
        copy(sum3.at[t], sum3.at[t], 5, {"shift": lax.rem(t + k, COLS)}).start()

    over(COLS, spread4)
    total(5, sum3, COLS - 1).wait_recv()
    whole = jnp.concatenate([sum3[a] for a in range(16)], 0)
    factor2 = lower_inverse(whole)
    basis_ref[...] = jnp.dot(factor2, mapped2, precision=HIGHEST, preferred_element_type=F32)

    total(0, land1, ROWS - 1).wait_send()
    total(1, map1, ROWS // 2 - 1).wait_send()
    total(2, land2, COLS - 1).wait_send()
    total(3, sum2, COLS - 1).wait_send()
    total(4, land3, ROWS - 1).wait_send()
    total(5, sum3, COLS - 1).wait_send()


def per_device(snapshots, tail_sensors, shift_offsets, start_basis):
    own = snapshots.transpose(1, 0, 2)
    tail = tail_sensors.transpose(1, 0, 2)
    offs = jnp.pad(shift_offsets, (0, BLOCK - shift_offsets.shape[0])).reshape(1, BLOCK)
    vmem = pl.BlockSpec(memory_space=pltpu.VMEM)
    smem = pl.BlockSpec(memory_space=pltpu.SMEM)
    dma = pltpu.SemaphoreType.DMA
    got, every_offs = pl.pallas_call(
        gather_kernel,
        out_shape=(
            jax.ShapeDtypeStruct((9, 2, BLOCK, SNAPS), BF16),
            jax.ShapeDtypeStruct((COLS, 1, BLOCK), jnp.int32),
        ),
        in_specs=[vmem] * 3,
        out_specs=(vmem, vmem),
        scratch_shapes=[dma((2, ROWS)), dma((3,)), dma((9,)), dma, dma],
        compiler_params=pltpu.CompilerParams(collective_id=0, has_side_effects=True),
        name="gather_sensors",
    )(own, tail, offs)
    f32 = lambda *shape: pltpu.VMEM(shape, F32)
    return pl.pallas_call(
        music_kernel,
        out_shape=(
            jax.ShapeDtypeStruct((BLOCK, 2 * BLOCK), F32),
            jax.ShapeDtypeStruct((K, BLOCK), F32),
        ),
        in_specs=[vmem, vmem, smem, vmem],
        out_specs=(vmem, vmem),
        scratch_shapes=[
            f32(2, 256, 128), f32(2, 256, 128), f32(2, 384, 128), f32(2, 384, 128), f32(128, 256),
            f32(16, 8, 128), f32(32, 8, 128), f32(16, 8, 128),
            f32(16, 8, 128), f32(16, 8, 128), f32(16, 8, 128),
            f32(16, 4, 128), f32(32, 4, 128), f32(16, 4, 128),
            dma((6,)), dma((6,)),
        ],
        compiler_params=pltpu.CompilerParams(collective_id=1, has_side_effects=True),
        name="music",
    )(own, got, every_offs, start_basis)


def solution(mesh):
    in_specs = (P("row", None, None), P(), P("shift"), P(None, "row"))
    out_specs = (P("row", "shift"), P(None, "row"))
    return jax.shard_map(per_device, mesh=mesh, in_specs=in_specs, out_specs=out_specs, check_vma=False)
```

time: 400 us -> 115 us (0.29)
  Pallas kernels: 0 us -> 109 us
  blocking collectives: 106 us -> 0 us
  loops' own time: 99.6 us -> 0 us
  waiting for transfers between devices: 58.6 us -> 0 us
  local copies, waits for them, and re-layouts: 47.8 us -> 4.89 us
  other arithmetic: 35.5 us -> 0 us
  matrix products: 19.8 us -> 0 us
  starting transfers between devices: 14.1 us -> 0 us
  between operations: 14.3 us -> 0.66 us
    pallas_call x0 -> x2, Pallas kernels: none -> 109 us  [the longest x1 65.8 us: per_device(): pl.pallas_call(music_kernel, out_shape=(jax.ShapeDtypeStruct((BLOCK, 2 *...]
    another operation x1 -> x0, loops' own time: 99.6 us -> none  [per_device(): lax.fori_loop(0, every_offset.shape[0], add_block, jnp.zeros((block_rows,...]
    all_to_all x2 -> x0, waiting for transfers between devices: 58.6 us -> none  [sent_to_all(): return lax.all_to_all(copies, axis, split_axis=0, concat_axis=0, tiled=True)]
    all_to_all x2 -> x0, blocking collectives: 53.7 us -> none  [sent_to_all(): return lax.all_to_all(copies, axis, split_axis=0, concat_axis=0, tiled=True)]
    all_gather x3 -> x0, blocking collectives: 52.4 us -> none  [the longest x2 41.1 us: total_of_pieces(): tiles = lax.all_gather(x, axis)]
    dynamic_slice x49 -> x0, local copies, waits for them, and re-layouts: 28.9 us -> none  [the longest x48 28.3 us: add_block(): offset = every_offset[which]]
    another operation x10 -> x0, other arithmetic: 24.1 us -> none  [the longest x6 13 us: factor(): lower_factor = jnp.linalg.cholesky(gram_matrix)]
    dot_general x54 -> x0, matrix products: 19.3 us -> none  [the longest x48 13.9 us: add_block(): lax.dot_general(own_rows, col_rows, (((1,), (1,)), ((), ())), preferred_e...]
  transfers between devices with their start and end apart: 3 -> 0, of which waited for: 2 -> 0; matrix products, arithmetic and copies ran while one was open for 1% -> 0% of each run, Pallas kernels for 0% -> 0%
where the time goes in v1:
time: 115 us
  Pallas kernels  109 us (95%)
  local copies, waits for them, and re-layouts  4.89 us (4%)
    pallas_call x1, Pallas kernels, per_device(): pl.pallas_call(music_kernel, out_shape=(jax.ShapeDtypeStruct((BLOCK, 2 *...  65.8 us
    pallas_call x1, Pallas kernels, per_device(): pl.pallas_call(gather_kernel, out_shape=(jax.ShapeDtypeStruct((9, 2, BLOC...  43.4 us

profile of v1, /device:TPU:1, one launch (start us, length us, event | category | flops | bytes accessed | tf_op | source)
XLA Modules:
  0.0 114.8 jit_solution(572594114155825944)
XLA Ops:
  0.6 1.2 %pad_bitcast_fusion.offs_ref = s32[1,128]{1,0:T(1,128)} fusion(s32[3]{0:T(128)} %param.6), kind=kLoop, calls=%fused_computation.2 | loop fusion | bytes 524 | tf_op jit(solution)/shard_map/reshape | solution.py:368
  1.8 1.5 %copy_bitcast_fusion = (bf16[2,128,128]{2,1,0:T(8,128)(2,1)}, bf16[2,128,128]{2,1,0:T(8,128)(2,1)}) fusion(bf16[128,2,128]{2,1,0:T(2,128)(2,1)} %param.5, bf16[128,2,128]{2,1,0:T(2,128)(2,1)} %param.4), kind=kLoop, calls=%fused_computation | loop fusion | bytes 262144 | tf_op jit(solution)/shard_map/transpose | solution.py:367
  3.3 43.4 %gather_sensors.1 = (bf16[9,2,128,128]{3,2,1,0:T(8,128)(2,1)}, s32[16,1,128]{2,1,0:T(1,128)}) custom-call(bf16[2,128,128]{2,1,0:T(8,128)(2,1)} %get-tuple-element.7.own_ref, bf16[2,128,128]{2,1,0:T(8,128)(2,1)} %get-tuple-element.6.tail_ref, s32[1,128]{1,0:T(1,128)} %pad_bitcast_fusion.offs_ref), custom_call_target="tpu_custom_call" | custom-call | tf_op jit(solution)/shard_map/gather_sensors/pallas_call | solution.py:372
  46.8 65.8 %music.1 = (f32[128,256]{1,0:T(8,128)}, f32[64,128]{1,0:T(8,128)}) custom-call(bf16[2,128,128]{2,1,0:T(8,128)(2,1)} %get-tuple-element.7.own_ref, bf16[9,2,128,128]{3,2,1,0:T(8,128)(2,1)} %get-tuple-element.4.got_ref, s32[16,1,128]{2,1,0:T(1,128)} %get-tuple-element.5.offs_ref, f32[64,128]{1,0:T(8,128)} %start_ref.1), custom_call_target="tpu_custom_call" | custom-call | tf_op jit(solution)/shard_map/music/pallas_call | solution.py:385
  112.6 0.0 copy-start
  112.6 1.6 %copy.12 = f32[128,256]{1,0:T(8,128)} copy(f32[128,256]{1,0:T(8,128)} %get-tuple-element.10) | data formatting | bytes 262144
  114.1 0.0 copy-done
  114.2 0.6 copy.13
Async XLA Ops:
  112.6 1.6 %copy-start = (f32[64,128]{1,0:T(8,128)S(1)}, f32[64,128]{1,0:T(8,128)}, u32[]{:S(2)}) copy-start(f32[64,128]{1,0:T(8,128)} %get-tuple-element.11) | copy-start | bytes 98308

commit v2 on v1

v2 whole, which is shorter than its diff:
```python
import jax
import jax.numpy as jnp
from jax import lax
from jax.experimental import pallas as pl
from jax.experimental.pallas import tpu as pltpu
from jax.sharding import PartitionSpec as P

M = 4096
K = 64
SNAPS = 128
SHIFTS = 48
ROWS = 32
COLS = 16
BLOCK = 128
HALF_ROOT = 0.7071067811865476
MESH = pl.DeviceIdType.MESH
HIGHEST = lax.Precision.HIGHEST
F32 = jnp.float32
BF16 = jnp.bfloat16


def signal_peers(barrier, r, t):
    def plane(k, _):
        pl.semaphore_signal(
            barrier, inc=1, device_id={"row": lax.rem(r + k, ROWS)}, device_id_type=MESH
        )
        return _

    def line(k, _):
        pl.semaphore_signal(
            barrier, inc=1, device_id={"shift": lax.rem(t + k, COLS)}, device_id_type=MESH
        )
        return _

    lax.fori_loop(1, ROWS, plane, 0)
    lax.fori_loop(1, COLS, line, 0)


def lower_inverse(gram):
    lanes = lax.broadcasted_iota(jnp.int32, (8, 128), 1)
    subs = lax.broadcasted_iota(jnp.int32, (8, 128), 0)
    rows = [gram[8 * i : 8 * i + 8] + jnp.where(lanes == subs + 8 * i, 1.0, 0.0) for i in range(8)]
    out = []
    for b in range(8):
        cols = [
            {i: jnp.broadcast_to(rows[i][:, 64 + 8 * b + j : 65 + 8 * b + j], (8, 128)) for i in range(b, 8)}
            for j in range(8)
        ]
        scale = jnp.zeros((8, 128), F32)
        for j in range(8):
            pivot = jnp.broadcast_to(cols[j][b][j : j + 1], (8, 128))
            root = lax.rsqrt(pivot)
            inverse = root * root
            scale = jnp.where(subs == j, root, scale)
            lead = jnp.broadcast_to(rows[b][j : j + 1], (8, 128))
            heads = {l: jnp.broadcast_to(cols[l][b][j : j + 1], (8, 128)) for l in range(j + 1, 8)}
            for i in range(b, 8):
                factor = cols[j][i] * inverse
                if i == b:
                    factor = jnp.where(subs > j, factor, 0.0)
                rows[i] = rows[i] - factor * lead
                for l in range(j + 1, 8):
                    cols[l][i] = cols[l][i] - factor * heads[l]
        out.append(rows[b] * scale)
    return jnp.concatenate(out, 0)[:, :64]


def padded_gram(x):
    both = jnp.concatenate([jnp.zeros_like(x), x], 0)
    return lax.dot_general(x, both, (((1,), (1,)), ((), ())), precision=HIGHEST, preferred_element_type=F32)


def selection(top, flipped):
    out = lax.broadcasted_iota(jnp.int32, (2 * BLOCK, 2 * BLOCK), 0)
    src = lax.broadcasted_iota(jnp.int32, (2 * BLOCK, 2 * BLOCK), 1)
    second = out >= BLOCK
    sensor = jnp.where(second, out - BLOCK, out)
    if flipped:
        sensor = BLOCK - 1 - sensor
    straight = jnp.where(second, 2 * sensor + 1, 2 * sensor)
    crossed = jnp.where(second, 2 * sensor, 2 * sensor + 1)
    minus = second if not flipped else jnp.logical_not(second)
    upper = jnp.where(src == straight, 1.0, 0.0)
    lower = jnp.where(src == crossed, jnp.where(minus, -1.0, 1.0), 0.0)
    return jnp.where(top, upper, lower).astype(BF16)


def music_kernel(
    own_ref, tail_ref, offs_ref, start_ref, cov_ref, basis_ref,
    got, picks, offs_all, offs_near, offs_now,
    row_w, row_m, col_w, col_m, acc,
    part1, land1, map1, part2, land2, sum2, part3, land3, sum3,
    wide_send, wide_recv, near_send, near_recv, offs_send, offs_recv, local_sem,
    send_sem, recv_sem,
):
    r = lax.axis_index("row")
    t = lax.axis_index("shift")
    x, y = r // 8, r % 8
    core = t % 2
    barrier = pltpu.get_barrier_semaphore()
    signal_peers(barrier, r, t)

    lane = lax.broadcasted_iota(jnp.int32, (1, BLOCK), 1)
    offs_near[...] = jnp.where(lane == 0, offs_ref[0], jnp.where(lane == 1, offs_ref[1], offs_ref[2]))
    row_top, col_top = r < ROWS // 2, t < COLS // 2
    picks[0] = selection(row_top, False)
    picks[1] = selection(row_top, True)
    picks[2] = selection(col_top, False)
    picks[3] = selection(col_top, True)
    acc[...] = jnp.zeros_like(acc)
    pl.semaphore_wait(barrier, ROWS - 1 + COLS - 1)

    def wide(src, slot, k, dest):
        return pltpu.make_async_remote_copy(
            src_ref=src,
            dst_ref=got.at[slot],
            send_sem=wide_send.at[slot - 3, k],
            recv_sem=wide_recv.at[slot - 3],
            device_id={"row": dest},
            device_id_type=MESH,
        )

    slots = []
    for group, first in enumerate((2 * t, 30 - 2 * t)):
        for place in range(3):
            block = first + place
            inside = block < ROWS
            bx, by = block // 8, block % 8
            source = block == r
            column = inside & (x == bx) & (y != by)
            opposite = inside & (x == (bx + 2) % 4) & (y == by)
            slots.append((3 + 3 * group + place, block, source, column, opposite))

    def along_y(src, slot):
        def step(i, c):
            far = 4 + ((i + 1) // 2) * (1 - 2 * (i % 2))
            wide(src, slot, i, x * 8 + (y + far) % 8).start()
            return c

        lax.fori_loop(0, 7, step, 0)

    def along_x(src, slot):
        wide(src, slot, 8, ((x + 1) % 4) * 8 + y).start()
        wide(src, slot, 9, ((x + 3) % 4) * 8 + y).start()

    for slot, block, source, column, opposite in slots:
        @pl.when(source)
        def _():
            wide(own_ref, slot, 7, ((x + 2) % 4) * 8 + y).start()
            along_y(own_ref, slot)
            along_x(own_ref, slot)

    def offs_copy(k):
        return pltpu.make_async_remote_copy(
            src_ref=offs_near,
            dst_ref=offs_all.at[t],
            send_sem=offs_send,
            recv_sem=offs_recv,
            device_id={"shift": (t + k) % COLS},
            device_id_type=MESH,
        )

    def send_offs(k, c):
        offs_copy(k).start()
        return c

    lax.fori_loop(1, COLS, send_offs, 0)
    offs_all[t] = offs_near[...]

    half = pl.ds(pl.multiple_of(core * BLOCK, BLOCK), BLOCK)
    other = pl.ds(pl.multiple_of((1 - core) * BLOCK, BLOCK), BLOCK)

    def near(slot, dest):
        return pltpu.make_async_remote_copy(
            src_ref=own_ref.at[half],
            dst_ref=got.at[slot, half],
            send_sem=near_send.at[slot, 0],
            recv_sem=near_recv.at[slot, 0],
            device_id={"row": dest},
            device_id_type=MESH,
        )

    def pass_on(slot, part):
        return pltpu.make_async_remote_copy(
            src_ref=got.at[slot, part],
            dst_ref=got.at[slot, part],
            send_sem=near_send.at[slot, 1],
            recv_sem=near_recv.at[slot, 1],
            device_id={"shift": t + 1 - 2 * core},
            device_id_type=MESH,
        )

    sends_near = (r >= 1, None, (r >= 1) & (r != 16))
    gets_near = (r != 31, None, (r != 0) & (r != 16))

    def when(condition, body):
        if condition is None:
            body()
        else:
            pl.when(condition)(body)

    for slot, dest in enumerate((r - 1, 31 - r, 32 - r)):
        when(sends_near[slot], lambda: near(slot, dest).start())

    for slot, block, source, column, opposite in slots:
        @pl.when(source)
        def _():
            got[slot] = own_ref[...]

    def from_tail(slot):
        def body():
            got[slot] = tail_ref[...]

        return body

    pl.when(r == 31)(from_tail(0))
    pl.when(r == 0)(from_tail(2))
    pl.when(t == 15)(from_tail(5))
    pl.when(t == 0)(from_tail(8))

    @pl.when(r == 16)
    def _():
        got[2] = own_ref[...]

    def put(window, pick, place, block):
        both = jnp.dot(picks[pick], block, preferred_element_type=F32) * HALF_ROOT
        window[0, pl.ds(place * BLOCK, BLOCK), :] = both[:BLOCK]
        window[1, pl.ds(place * BLOCK, BLOCK), :] = both[BLOCK:]

    put(row_w, 0, 0, own_ref[...])

    for slot, block, source, column, opposite in slots:
        @pl.when(opposite)
        def _():
            wide(own_ref, slot, 0, r).wait_recv()
            along_y(got.at[slot], slot)

    for slot, block, source, column, opposite in slots:
        @pl.when(column)
        def _():
            wide(own_ref, slot, 0, r).wait_recv()
            along_x(got.at[slot], slot)

    for slot in range(3):
        def body():
            near(slot, r).wait_recv()
            pass_on(slot, half).start()

        when(gets_near[slot], body)

    every_offs = offs_all.at[pl.ds(0, COLS - 1)]
    whole_offs = pltpu.make_async_remote_copy(
        src_ref=every_offs,
        dst_ref=every_offs,
        send_sem=offs_send,
        recv_sem=offs_recv,
        device_id={"row": r},
        device_id_type=MESH,
    )
    whole_offs.wait_recv()
    to_scalar = pltpu.make_async_copy(offs_all, offs_now, local_sem)
    to_scalar.start()

    for slot in range(3):
        when(gets_near[slot], lambda: pass_on(slot, other).wait_recv())
    put(row_w, 0, 1, got[0])
    put(row_m, 1, 0, got[2])
    put(row_m, 1, 1, got[1])

    for slot, block, source, column, opposite in slots:
        waits = (block < ROWS) & jnp.logical_not(source | column | opposite)
        pl.when(waits)(lambda: wide(own_ref, slot, 0, r).wait_recv())
    for place in range(3):
        put(col_w, 2, place, got[3 + place])
        put(col_m, 3, place, got[8 - place])
    to_scalar.wait()

    def pairs(window, mirror, offset, count):
        parts = []
        for c in range(2):
            a = window[c, pl.ds(offset, count), :]
            b = mirror[c, pl.ds(BLOCK - offset, count), :]
            parts.append((a + b).astype(BF16))
        return parts

    def some(i, c):
        lhs, rhs = [], []
        for j in range(3):
            offset = offs_now[i, 0, j]
            lhs += pairs(row_w, row_m, offset, BLOCK)
            rhs += pairs(col_w, col_m, offset, 2 * BLOCK)
        acc[...] += lax.dot_general(
            jnp.concatenate(lhs, 1), jnp.concatenate(rhs, 1), (((1,), (1,)), ((), ())), preferred_element_type=F32
        )
        return c

    lax.fori_loop(0, COLS, some, 0)
    cov = acc[...] * (1.0 / (SNAPS * SHIFTS))
    cov_ref[...] = cov

    first = jnp.dot(start_ref[...], cov, precision=HIGHEST, preferred_element_type=F32)
    for c in range(2):
        for a in range(16):
            part1[16 * c + a] = first[4 * a : 4 * a + 4, BLOCK * c : BLOCK * c + BLOCK]

    def copy(src, dst, phase, where):
        return pltpu.make_async_remote_copy(
            src_ref=src,
            dst_ref=dst,
            send_sem=send_sem.at[phase],
            recv_sem=recv_sem.at[phase],
            device_id=where,
            device_id_type=MESH,
        )

    def over(count, body):
        def step(k, c):
            body(k)
            return c

        lax.fori_loop(1, count, step, 0)

    def total(phase, buffer, count):
        every = buffer.at[pl.ds(0, count)]
        return copy(every, every, phase, {"row": r})

    def scatter1(k):
        dest = lax.rem(r + k, ROWS)
        copy(part1.at[dest], land1.at[r], 0, {"row": dest}).start()

    over(ROWS, scatter1)
    land1[r] = part1[r]
    total(0, land1, ROWS - 1).wait_recv()
    map1[r] = jnp.sum(land1[...], axis=0)

    def spread1(k):
        copy(map1.at[r], map1.at[r], 1, {"row": (r + k) % ROWS}).start()

    over(ROWS, spread1)
    total(1, map1, ROWS - 1).wait_recv()
    mapped = jnp.concatenate(
        [jnp.concatenate([map1[16 * c + a] for a in range(16)], 0) for c in range(2)], 1
    )

    gram1 = padded_gram(mapped)
    second = lax.dot_general(
        mapped, cov_ref[...], (((1,), (1,)), ((), ())), precision=HIGHEST, preferred_element_type=F32
    )
    for a in range(8):
        part2[a] = second[8 * a : 8 * a + 8]
        part2[8 + a] = gram1[8 * a : 8 * a + 8]

    def scatter2(k):
        dest = lax.rem(t + k, COLS)
        copy(part2.at[dest], land2.at[t], 2, {"shift": dest}).start()

    over(COLS, scatter2)
    land2[t] = part2[t]
    total(2, land2, COLS - 1).wait_recv()
    sum2[t] = jnp.sum(land2[...], axis=0)

    def spread2(k):
        copy(sum2.at[t], sum2.at[t], 3, {"shift": lax.rem(t + k, COLS)}).start()

    over(COLS, spread2)
    total(3, sum2, COLS - 1).wait_recv()
    factor1 = lower_inverse(sum2[8:16].reshape(K, BLOCK))
    mapped2 = jnp.dot(factor1, sum2[0:8].reshape(K, BLOCK), precision=HIGHEST, preferred_element_type=F32)
    gram2 = padded_gram(mapped2)
    for a in range(16):
        part3[a] = gram2[4 * a : 4 * a + 4]

    def spread3(k):
        copy(part3.at[t], land3.at[r], 4, {"row": lax.rem(r + k, ROWS)}).start()

    over(ROWS, spread3)
    land3[r] = part3[t]
    total(4, land3, ROWS - 1).wait_recv()
    sum3[t] = jnp.sum(land3[...], axis=0)

    def spread4(k):
        copy(sum3.at[t], sum3.at[t], 5, {"shift": lax.rem(t + k, COLS)}).start()

    over(COLS, spread4)
    total(5, sum3, COLS - 1).wait_recv()
    whole = jnp.concatenate([sum3[a] for a in range(16)], 0)
    factor2 = lower_inverse(whole)
    basis_ref[...] = jnp.dot(factor2, mapped2, precision=HIGHEST, preferred_element_type=F32)

    for slot, block, source, column, opposite in slots:
        def drain(low, high):
            def done(k, c):
                wide(own_ref, slot, k, r).wait_send()
                return c

            lax.fori_loop(low, high, done, 0)

        pl.when(source)(lambda: drain(0, 10))
        pl.when(column)(lambda: drain(8, 10))
        pl.when(opposite)(lambda: drain(0, 7))
    for slot in range(3):
        when(sends_near[slot], lambda: near(slot, r).wait_send())
        when(gets_near[slot], lambda: pass_on(slot, half).wait_send())
    whole_offs.wait_send()
    total(0, land1, ROWS - 1).wait_send()
    total(1, map1, ROWS - 1).wait_send()
    total(2, land2, COLS - 1).wait_send()
    total(3, sum2, COLS - 1).wait_send()
    total(4, land3, ROWS - 1).wait_send()
    total(5, sum3, COLS - 1).wait_send()


def per_device(snapshots, tail_sensors, shift_offsets, start_basis):
    own = snapshots.reshape(2 * BLOCK, SNAPS)
    tail = tail_sensors.reshape(2 * BLOCK, SNAPS)
    vmem = pl.BlockSpec(memory_space=pltpu.VMEM)
    smem = pl.BlockSpec(memory_space=pltpu.SMEM)
    dma = pltpu.SemaphoreType.DMA
    f32 = lambda *shape: pltpu.VMEM(shape, F32)
    return pl.pallas_call(
        music_kernel,
        out_shape=(
            jax.ShapeDtypeStruct((BLOCK, 2 * BLOCK), F32),
            jax.ShapeDtypeStruct((K, BLOCK), F32),
        ),
        in_specs=[vmem, vmem, smem, vmem],
        out_specs=(vmem, vmem),
        scratch_shapes=[
            pltpu.VMEM((9, 256, 128), BF16), pltpu.VMEM((4, 256, 256), BF16),
            pltpu.VMEM((COLS, 1, BLOCK), jnp.int32), pltpu.VMEM((1, BLOCK), jnp.int32),
            pltpu.SMEM((COLS, 1, BLOCK), jnp.int32),
            f32(2, 256, 128), f32(2, 256, 128), f32(2, 384, 128), f32(2, 384, 128), f32(128, 256),
            f32(32, 4, 128), f32(32, 4, 128), f32(32, 4, 128),
            f32(16, 8, 128), f32(16, 8, 128), f32(16, 8, 128),
            f32(16, 4, 128), f32(32, 4, 128), f32(16, 4, 128),
            dma((6, 10)), dma((6,)), dma((3, 2)), dma((3, 2)), dma, dma, dma,
            dma((6,)), dma((6,)),
        ],
        compiler_params=pltpu.CompilerParams(collective_id=0, has_side_effects=True),
        name="music",
    )(own, tail, shift_offsets, start_basis)


def solution(mesh):
    in_specs = (P("row", None, None), P(), P("shift"), P(None, "row"))
    out_specs = (P("row", "shift"), P(None, "row"))
    return jax.shard_map(per_device, mesh=mesh, in_specs=in_specs, out_specs=out_specs, check_vma=False)
```

time: 115 us -> 80.5 us (0.70)
  Pallas kernels: 109 us -> 77.6 us
  local copies, waits for them, and re-layouts: 4.89 us -> 2.19 us
    pallas_call x1 -> x0, Pallas kernels: 43.4 us -> none  [per_device(): pl.pallas_call(gather_kernel, out_shape=(jax.ShapeDtypeStruct((9, 2, BLOC...]
    pallas_call x1, Pallas kernels: 65.8 us -> 77.6 us  [per_device(): pl.pallas_call(music_kernel, out_shape=(jax.ShapeDtypeStruct((BLOCK, 2 *...]
    transpose x1 -> x0, local copies, waits for them, and re-layouts: 1.53 us -> none  [per_device(): tail = tail_sensors.transpose(1, 0, 2)]
    reshape x1 -> x0, local copies, waits for them, and re-layouts: 1.17 us -> none  [per_device(): jnp.pad(shift_offsets, (0, BLOCK - shift_offsets.shape[0]))]
where the time goes in v2:
time: 80.5 us; the launch traced here: 80.4 us
  Pallas kernels  77.6 us (96%)
  local copies, waits for them, and re-layouts  2.19 us (3%)
    pallas_call x1, Pallas kernels, per_device(): pl.pallas_call(music_kernel, out_shape=(jax.ShapeDtypeStruct((BLOCK, 2 *...  77.6 us
    unnamed x4, local copies, waits for them, and re-layouts  2.19 us

profile of v2, /device:TPU:1, one launch (start us, length us, event | category | flops | bytes accessed | tf_op | source)
XLA Modules:
  0.0 80.4 jit_solution(14451016511597980529)
XLA Ops:
  0.6 77.6 %music.1 = (f32[128,256]{1,0:T(8,128)}, f32[64,128]{1,0:T(8,128)}) custom-call(bf16[256,128]{1,0:T(8,128)(2,1)} %bitcast.2, bf16[256,128]{1,0:T(8,128)(2,1)} %bitcast.3, s32[3]{0:T(128)} %offs_ref.1, f32[64,128]{1,0:T(8,128)} %start_ref.1), custom_call_target="tpu_custom_call" | custom-call | tf_op jit(solution)/shard_map/music/pallas_call | solution.py:420
  78.2 0.0 copy-start
  78.2 1.6 %copy.8 = f32[128,256]{1,0:T(8,128)} copy(f32[128,256]{1,0:T(8,128)} %get-tuple-element.4) | data formatting | bytes 262144
  79.8 0.0 copy-done
  79.8 0.6 copy.9
Async XLA Ops:
  78.2 1.6 %copy-start = (f32[64,128]{1,0:T(8,128)S(1)}, f32[64,128]{1,0:T(8,128)}, u32[]{:S(2)}) copy-start(f32[64,128]{1,0:T(8,128)} %get-tuple-element.5) | copy-start | bytes 98308

commit v3 on v2

--- a/solution.py
+++ b/solution.py
@@ -285,8 +285,8 @@
 
     def some(i, c):
         lhs, rhs = [], []
-        for j in range(3):
-            offset = offs_now[i, 0, j]
+        for j in range(12):
+            offset = offs_now[i * 4 + j // 3, 0, j % 3]
             lhs += pairs(row_w, row_m, offset, BLOCK)
             rhs += pairs(col_w, col_m, offset, 2 * BLOCK)
         acc[...] += lax.dot_general(
@@ -294,7 +294,7 @@
         )
         return c
 
-    lax.fori_loop(0, COLS, some, 0)
+    lax.fori_loop(0, 4, some, 0)
     cov = acc[...] * (1.0 / (SNAPS * SHIFTS))
     cov_ref[...] = cov
 
@@ -420,8 +420,8 @@
     return pl.pallas_call(
         music_kernel,
         out_shape=(
-            jax.ShapeDtypeStruct((BLOCK, 2 * BLOCK), F32),
-            jax.ShapeDtypeStruct((K, BLOCK), F32),
+            pltpu.VMEM((BLOCK, 2 * BLOCK), F32),
+            pltpu.VMEM((K, BLOCK), F32),
         ),
         in_specs=[vmem, vmem, smem, vmem],
         out_specs=(vmem, vmem),

time: 80.5 us -> 77.1 us (0.958)
  Pallas kernels: 77.6 us -> 74.9 us
  local copies, waits for them, and re-layouts: 2.19 us -> 1.27 us
    pallas_call x1, Pallas kernels: 77.6 us -> 74.9 us  [per_device(): pl.pallas_call(music_kernel, out_shape=(pltpu.VMEM((BLOCK, 2 * BLOCK), F3...]
    unnamed x4 -> x2, local copies, waits for them, and re-layouts: 2.19 us -> 1.27 us
where the time goes in v3:
time: 77.1 us; the launch traced here: 76.9 us
  Pallas kernels  74.9 us (97%)
  local copies, waits for them, and re-layouts  1.27 us (2%)
    pallas_call x1, Pallas kernels, per_device(): pl.pallas_call(music_kernel, out_shape=(pltpu.VMEM((BLOCK, 2 * BLOCK), F3...  74.9 us

profile of v3, /device:TPU:1, one launch (start us, length us, event | category | flops | bytes accessed | tf_op | source)
XLA Modules:
  0.0 76.9 jit_solution(9975362123363474149)
XLA Ops:
  0.6 74.9 %music.1 = (f32[128,256]{1,0:T(8,128)S(1)}, f32[64,128]{1,0:T(8,128)S(1)}) custom-call(bf16[256,128]{1,0:T(8,128)(2,1)} %bitcast.2, bf16[256,128]{1,0:T(8,128)(2,1)} %bitcast.3, s32[3]{0:T(128)} %offs_ref.1, f32[64,128]{1,0:T(8,128)} %start_ref.1), custom_call_target="tpu_custom_call" | custom-call | tf_op jit(solution)/shard_map/music/pallas_call | solution.py:420
  75.6 0.7 copy.8
  76.2 0.6 copy.9

commit v4 on v3

v4 whole, which is shorter than its diff:
```python
import jax
import jax.numpy as jnp
from jax import lax
from jax.experimental import pallas as pl
from jax.experimental.pallas import tpu as pltpu
from jax.sharding import PartitionSpec as P

M = 4096
K = 64
SNAPS = 128
SHIFTS = 48
ROWS = 32
COLS = 16
BLOCK = 128
HALF_ROOT = 0.7071067811865476
MESH = pl.DeviceIdType.MESH
HIGHEST = lax.Precision.HIGHEST
F32 = jnp.float32
BF16 = jnp.bfloat16


def far_first(n):
    return sorted(range(n), key=lambda d: -min(d, n - d))


def plane_peers(r):
    x, y = lax.div(r, 8), lax.rem(r, 8)
    xs = [lax.rem(x + a, 4) * 8 for a in range(4)]
    ys = [lax.rem(y + b, 8) for b in range(8)]
    order = sorted(
        ((a, b) for a in range(4) for b in range(8) if a or b),
        key=lambda d: -min(d[0], 4 - d[0]) - min(d[1], 8 - d[1]),
    )
    return [xs[a] + ys[b] for a, b in order]


def line_peers(t):
    z, core = lax.div(t, 2), lax.rem(t, 2)
    zs = [lax.rem(z + a, 8) * 2 for a in range(8)]
    cores = [core, 1 - core]
    return [zs[a] + cores[b] for a in far_first(8) for b in (1, 0) if a or b]


def signal_peers(barrier, rows, places):
    for dest in rows:
        pl.semaphore_signal(barrier, inc=1, device_id={"row": dest}, device_id_type=MESH)
    for dest in places:
        pl.semaphore_signal(barrier, inc=1, device_id={"shift": dest}, device_id_type=MESH)


def lower_inverse(gram):
    lanes = lax.broadcasted_iota(jnp.int32, (8, 128), 1)
    subs = lax.broadcasted_iota(jnp.int32, (8, 128), 0)
    rows = [gram[8 * i : 8 * i + 8] + jnp.where(lanes == subs + 8 * i, 1.0, 0.0) for i in range(8)]
    out = []
    for b in range(8):
        cols = [
            {i: jnp.broadcast_to(rows[i][:, 64 + 8 * b + j : 65 + 8 * b + j], (8, 128)) for i in range(b, 8)}
            for j in range(8)
        ]
        scale = jnp.zeros((8, 128), F32)
        for l in range(8):
            cols[l][b] = jnp.where(lanes < 128 + subs, cols[l][b], 0.0)
        for j in range(8):
            root = jnp.broadcast_to(lax.rsqrt(cols[j][b])[j : j + 1], (8, 128))
            inverse = root * root
            scale = jnp.where(subs == j, root, scale)
            lead = jnp.broadcast_to(rows[b][j : j + 1], (8, 128))
            heads = {l: jnp.broadcast_to(cols[l][b][j : j + 1], (8, 128)) for l in range(j + 1, 8)}
            below = jnp.where(subs > j, cols[j][b], 0.0)
            for l in range(j + 1, 8):
                cols[l][b] = cols[l][b] - (below * heads[l]) * inverse
            rows[b] = rows[b] - (below * lead) * inverse
            for i in range(b + 1, 8):
                factor = cols[j][i] * inverse
                rows[i] = rows[i] - factor * lead
                for l in range(j + 1, 8):
                    cols[l][i] = cols[l][i] - factor * heads[l]
        out.append(rows[b] * scale)
    return jnp.concatenate(out, 0)[:, :64]


def padded_gram(x):
    both = jnp.concatenate([jnp.zeros_like(x), x], 0)
    return lax.dot_general(x, both, (((1,), (1,)), ((), ())), precision=HIGHEST, preferred_element_type=F32)


def selection(top, flipped):
    out = lax.broadcasted_iota(jnp.int32, (2 * BLOCK, 2 * BLOCK), 0)
    src = lax.broadcasted_iota(jnp.int32, (2 * BLOCK, 2 * BLOCK), 1)
    second = out >= BLOCK
    sensor = jnp.where(second, out - BLOCK, out)
    if flipped:
        sensor = BLOCK - 1 - sensor
    straight = jnp.where(second, 2 * sensor + 1, 2 * sensor)
    crossed = jnp.where(second, 2 * sensor, 2 * sensor + 1)
    minus = second if not flipped else jnp.logical_not(second)
    upper = jnp.where(src == straight, 1.0, 0.0)
    lower = jnp.where(src == crossed, jnp.where(minus, -1.0, 1.0), 0.0)
    return jnp.where(top, upper, lower).astype(BF16)


def music_kernel(
    own_any, tail_any, offs_ref, start_any, cov_ref, basis_ref,
    own_ref, tail_ref, start_ref,
    got, picks, offs_all, offs_near, offs_now,
    row_w, row_m, col_w, col_m, acc,
    part1, land1, map1, part2, land2, sum2, part3, land3, sum3,
    wide_send, wide_recv, pair_send, pair_recv, near_send, near_recv, offs_send, offs_recv, local_sem,
    send_sem, recv_sem,
):
    r = lax.axis_index("row")
    t = lax.axis_index("shift")
    x, y = lax.div(r, 8), lax.rem(r, 8)
    z, core = lax.div(t, 2), lax.rem(t, 2)
    rows, places = plane_peers(r), line_peers(t)
    column_rows = [x * 8 + lax.rem(y + b, 8) for b in far_first(8) if b]
    bring_own = pltpu.make_async_copy(own_any, own_ref, local_sem.at[1])
    bring_own.start()
    barrier = pltpu.get_barrier_semaphore()
    signal_peers(barrier, rows, places)
    bring_tail = pltpu.make_async_copy(tail_any, tail_ref, local_sem.at[2])
    bring_tail.start()
    bring_start = pltpu.make_async_copy(start_any, start_ref, local_sem.at[3])
    bring_start.start()

    lane = lax.broadcasted_iota(jnp.int32, (1, BLOCK), 1)
    offs_near[...] = jnp.where(lane == 0, offs_ref[0], jnp.where(lane == 1, offs_ref[1], offs_ref[2]))
    half = pl.ds(pl.multiple_of(core * BLOCK, BLOCK), BLOCK)
    other = pl.ds(pl.multiple_of((1 - core) * BLOCK, BLOCK), BLOCK)
    piece = pl.ds(pl.multiple_of(t * 16, 16), 16)
    bring_own.wait()
    pl.semaphore_wait(barrier, ROWS - 1 + COLS - 1)

    slots = []
    for group in range(2):
        if group == 0:
            blocks = (4 * z + 2, 2 * t + 1, 4 * z + 4 * core)
        else:
            blocks = (30 - 4 * z, 31 - 2 * t, 32 - 4 * z - 4 * core)
        for place, block in enumerate(blocks):
            inside = block < ROWS
            bx, by = lax.div(block, 8), lax.rem(block, 8)
            source = block == r
            column = inside & (x == bx) & (y != by)
            opposite = inside & (x == lax.rem(bx + 2, 4)) & (y == by)
            slots.append((3 + 3 * group + place, block, source, column, opposite))

    def shared(slot):
        return slot % 3 == 0

    def wide(slot, k, dest, from_own=False):
        src, dst = own_ref if from_own else got.at[slot], got.at[slot]
        if shared(slot):
            src, dst = src.at[half], dst.at[half]
        return pltpu.make_async_remote_copy(
            src_ref=src,
            dst_ref=dst,
            send_sem=wide_send.at[slot - 3, k],
            recv_sem=wide_recv.at[slot - 3],
            device_id={"row": dest},
            device_id_type=MESH,
        )

    def pair(slot, part):
        return pltpu.make_async_remote_copy(
            src_ref=got.at[slot, part],
            dst_ref=got.at[slot, part],
            send_sem=pair_send.at[slot // 3 - 1],
            recv_sem=pair_recv.at[slot // 3 - 1],
            device_id={"shift": t + 1 - 2 * core},
            device_id_type=MESH,
        )

    def along_y(slot, from_own=False):
        for i, dest in enumerate(column_rows):
            wide(slot, i, dest, from_own).start()

    def along_x(slot, from_own=False):
        wide(slot, 8, lax.rem(x + 1, 4) * 8 + y, from_own).start()
        wide(slot, 9, lax.rem(x + 3, 4) * 8 + y, from_own).start()

    for slot, block, source, column, opposite in slots:
        @pl.when(source)
        def _():
            wide(slot, 7, lax.rem(x + 2, 4) * 8 + y, True).start()
            along_y(slot, True)
            along_x(slot, True)

    def near(slot, dest):
        return pltpu.make_async_remote_copy(
            src_ref=own_ref.at[piece],
            dst_ref=got.at[slot, piece],
            send_sem=near_send.at[slot, 0],
            recv_sem=near_recv.at[slot, 0],
            device_id={"row": dest},
            device_id_type=MESH,
        )

    def pass_on(slot, part, dest):
        return pltpu.make_async_remote_copy(
            src_ref=got.at[slot, part],
            dst_ref=got.at[slot, part],
            send_sem=near_send.at[slot, 1],
            recv_sem=near_recv.at[slot, 1],
            device_id={"shift": dest},
            device_id_type=MESH,
        )

    sends_near = (r >= 1, None, (r >= 1) & (r != 16))
    gets_near = (r != 31, None, (r != 0) & (r != 16))

    def when(condition, body):
        if condition is None:
            body()
        else:
            pl.when(condition)(body)

    for slot, dest in enumerate((r - 1, 31 - r, 32 - r)):
        when(sends_near[slot], lambda: near(slot, dest).start())

    def offs_copy(dest):
        return pltpu.make_async_remote_copy(
            src_ref=offs_near,
            dst_ref=offs_all.at[t],
            send_sem=offs_send,
            recv_sem=offs_recv,
            device_id={"shift": dest},
            device_id_type=MESH,
        )

    for dest in places:
        offs_copy(dest).start()
    offs_all[t] = offs_near[...]

    for slot, block, source, column, opposite in slots:
        @pl.when(opposite)
        def _():
            wide(slot, 0, r).wait_recv()
            along_y(slot)

    for slot in range(3):
        def body():
            near(slot, r).wait_recv()

            for dest in places:
                pass_on(slot, piece, dest).start()

        when(gets_near[slot], body)

    for slot, block, source, column, opposite in slots:
        @pl.when(column)
        def _():
            wide(slot, 0, r).wait_recv()
            along_x(slot)

    for slot, block, source, column, opposite in slots:
        if shared(slot):
            waits = jnp.logical_not(source | column | opposite)
            pl.when(waits)(lambda: wide(slot, 0, r).wait_recv())
            pl.when(jnp.logical_not(source))(lambda: pair(slot, half).start())

    picks[0] = selection(r < ROWS // 2, False)
    picks[1] = selection(r < ROWS // 2, True)
    picks[2] = selection(t < COLS // 2, False)
    picks[3] = selection(t < COLS // 2, True)
    acc[...] = jnp.zeros_like(acc)
    bring_tail.wait()
    bring_start.wait()

    for slot, block, source, column, opposite in slots:
        @pl.when(source)
        def _():
            got[slot] = own_ref[...]

    def from_tail(slot):
        def body():
            got[slot] = tail_ref[...]

        return body

    pl.when(r == 31)(from_tail(0))
    pl.when(r == 0)(from_tail(2))
    pl.when(t == 15)(from_tail(5))
    pl.when(t == 0)(from_tail(8))

    @pl.when(r == 16)
    def _():
        got[2] = own_ref[...]

    def put(window, pick, place, block):
        both = jnp.dot(picks[pick], block, preferred_element_type=F32) * HALF_ROOT
        window[0, pl.ds(place * BLOCK, BLOCK), :] = both[:BLOCK]
        window[1, pl.ds(place * BLOCK, BLOCK), :] = both[BLOCK:]

    put(row_w, 0, 0, own_ref[...])

    every_offs = offs_all.at[pl.ds(0, COLS - 1)]
    whole_offs = pltpu.make_async_remote_copy(
        src_ref=every_offs,
        dst_ref=every_offs,
        send_sem=offs_send,
        recv_sem=offs_recv,
        device_id={"row": r},
        device_id_type=MESH,
    )
    whole_offs.wait_recv()
    to_scalar = pltpu.make_async_copy(offs_all, offs_now, local_sem.at[0])
    to_scalar.start()

    many = pl.ds(0, 16 * (COLS - 1))
    for slot in range(3):
        when(gets_near[slot], lambda: pass_on(slot, many, t).wait_recv())
    put(row_w, 0, 1, got[0])
    put(row_m, 1, 0, got[2])
    put(row_m, 1, 1, got[1])

    for slot, block, source, column, opposite in slots:
        if not shared(slot):
            waits = (block < ROWS) & jnp.logical_not(source | column | opposite)
            pl.when(waits)(lambda: wide(slot, 0, r).wait_recv())
    for slot, block, source, column, opposite in slots:
        if shared(slot):
            pl.when(jnp.logical_not(source))(lambda: pair(slot, other).wait_recv())
    low, high = 2 - 2 * core, 2 * core
    for place, (w, m) in enumerate(((3 + low, 6 + low), (4, 7), (3 + high, 6 + high))):
        put(col_w, 2, place, got[w])
        put(col_m, 3, place, got[m])
    to_scalar.wait()

    def pairs(window, mirror, offset, count):
        parts = []
        for c in range(2):
            a = window[c, pl.ds(offset, count), :]
            b = mirror[c, pl.ds(BLOCK - offset, count), :]
            parts.append((a + b).astype(BF16))
        return parts

    def some(i, c):
        lhs, rhs = [], []
        for j in range(12):
            offset = offs_now[i * 4 + j // 3, 0, j % 3]
            lhs += pairs(row_w, row_m, offset, BLOCK)
            rhs += pairs(col_w, col_m, offset, 2 * BLOCK)
        acc[...] += lax.dot_general(
            jnp.concatenate(lhs, 1), jnp.concatenate(rhs, 1), (((1,), (1,)), ((), ())), preferred_element_type=F32
        )
        return c

    lax.fori_loop(0, 4, some, 0)
    cov = acc[...] * (1.0 / (SNAPS * SHIFTS))
    cov_ref[...] = cov

    first = jnp.dot(start_ref[...], cov, precision=HIGHEST, preferred_element_type=F32)
    for c in range(2):
        for a in range(16):
            part1[16 * c + a] = first[4 * a : 4 * a + 4, BLOCK * c : BLOCK * c + BLOCK]

    def copy(src, dst, phase, where):
        return pltpu.make_async_remote_copy(
            src_ref=src,
            dst_ref=dst,
            send_sem=send_sem.at[phase],
            recv_sem=recv_sem.at[phase],
            device_id=where,
            device_id_type=MESH,
        )

    def total(phase, buffer, count):
        every = buffer.at[pl.ds(0, count)]
        return copy(every, every, phase, {"row": r})

    for dest in rows:
        copy(part1.at[dest], land1.at[r], 0, {"row": dest}).start()
    land1[r] = part1[r]
    total(0, land1, ROWS - 1).wait_recv()
    map1[r] = jnp.sum(land1[...], axis=0)

    for dest in rows:
        copy(map1.at[r], map1.at[r], 1, {"row": dest}).start()
    total(1, map1, ROWS - 1).wait_recv()
    mapped = jnp.concatenate(
        [jnp.concatenate([map1[16 * c + a] for a in range(16)], 0) for c in range(2)], 1
    )

    gram1 = padded_gram(mapped)
    second = lax.dot_general(
        mapped, cov_ref[...], (((1,), (1,)), ((), ())), precision=HIGHEST, preferred_element_type=F32
    )
    for a in range(8):
        part2[a] = second[8 * a : 8 * a + 8]
        part2[8 + a] = gram1[8 * a : 8 * a + 8]

    for dest in places:
        copy(part2.at[dest], land2.at[t], 2, {"shift": dest}).start()
    land2[t] = part2[t]
    total(2, land2, COLS - 1).wait_recv()
    sum2[t] = jnp.sum(land2[...], axis=0)

    for dest in places:
        copy(sum2.at[t], sum2.at[t], 3, {"shift": dest}).start()
    total(3, sum2, COLS - 1).wait_recv()
    factor1 = lower_inverse(sum2[8:16].reshape(K, BLOCK))
    mapped2 = jnp.dot(factor1, sum2[0:8].reshape(K, BLOCK), precision=HIGHEST, preferred_element_type=F32)
    gram2 = padded_gram(mapped2)
    for a in range(16):
        part3[a] = gram2[4 * a : 4 * a + 4]

    for dest in rows:
        copy(part3.at[t], land3.at[r], 4, {"row": dest}).start()
    land3[r] = part3[t]
    total(4, land3, ROWS - 1).wait_recv()
    sum3[t] = jnp.sum(land3[...], axis=0)

    for dest in places:
        copy(sum3.at[t], sum3.at[t], 5, {"shift": dest}).start()
    total(5, sum3, COLS - 1).wait_recv()
    whole = jnp.concatenate([sum3[a] for a in range(16)], 0)
    factor2 = lower_inverse(whole)
    basis_ref[...] = jnp.dot(factor2, mapped2, precision=HIGHEST, preferred_element_type=F32)

    for slot, block, source, column, opposite in slots:
        def drain(low, high):
            def done(k, c):
                wide(slot, k, r).wait_send()
                return c

            lax.fori_loop(low, high, done, 0)

        pl.when(source)(lambda: drain(0, 10))
        pl.when(column)(lambda: drain(8, 10))
        pl.when(opposite)(lambda: drain(0, 7))
        if shared(slot):
            pl.when(jnp.logical_not(source))(lambda: pair(slot, half).wait_send())
    for slot in range(3):
        when(sends_near[slot], lambda: near(slot, r).wait_send())
        when(gets_near[slot], lambda: pass_on(slot, many, t).wait_send())
    whole_offs.wait_send()
    total(0, land1, ROWS - 1).wait_send()
    total(1, map1, ROWS - 1).wait_send()
    total(2, land2, COLS - 1).wait_send()
    total(3, sum2, COLS - 1).wait_send()
    total(4, land3, ROWS - 1).wait_send()
    total(5, sum3, COLS - 1).wait_send()


def per_device(snapshots, tail_sensors, shift_offsets, start_basis):
    own = snapshots.reshape(2 * BLOCK, SNAPS)
    tail = tail_sensors.reshape(2 * BLOCK, SNAPS)
    vmem = pl.BlockSpec(memory_space=pltpu.VMEM)
    smem = pl.BlockSpec(memory_space=pltpu.SMEM)
    hbm = pl.BlockSpec(memory_space=pl.ANY)
    dma = pltpu.SemaphoreType.DMA
    f32 = lambda *shape: pltpu.VMEM(shape, F32)
    return pl.pallas_call(
        music_kernel,
        out_shape=(
            pltpu.VMEM((BLOCK, 2 * BLOCK), F32),
            pltpu.VMEM((K, BLOCK), F32),
        ),
        in_specs=[hbm, hbm, smem, hbm],
        out_specs=(vmem, vmem),
        scratch_shapes=[
            pltpu.VMEM((256, 128), BF16), pltpu.VMEM((256, 128), BF16), f32(K, BLOCK),
            pltpu.VMEM((9, 256, 128), BF16), pltpu.VMEM((4, 256, 256), BF16),
            pltpu.VMEM((COLS, 1, BLOCK), jnp.int32), pltpu.VMEM((1, BLOCK), jnp.int32),
            pltpu.SMEM((COLS, 1, BLOCK), jnp.int32),
            f32(2, 256, 128), f32(2, 256, 128), f32(2, 384, 128), f32(2, 384, 128), f32(128, 256),
            f32(32, 4, 128), f32(32, 4, 128), f32(32, 4, 128),
            f32(16, 8, 128), f32(16, 8, 128), f32(16, 8, 128),
            f32(16, 4, 128), f32(32, 4, 128), f32(16, 4, 128),
            dma((6, 10)), dma((6,)), dma((2,)), dma((2,)), dma((3, 2)), dma((3, 2)), dma, dma, dma((4,)),
            dma((6,)), dma((6,)),
        ],
        compiler_params=pltpu.CompilerParams(collective_id=0, has_side_effects=True),
        name="music",
    )(own, tail, shift_offsets, start_basis)


def solution(mesh):
    in_specs = (P("row", None, None), P(), P("shift"), P(None, "row"))
    out_specs = (P("row", "shift"), P(None, "row"))
    return jax.shard_map(per_device, mesh=mesh, in_specs=in_specs, out_specs=out_specs, check_vma=False)
```

time: 77.1 us -> 73.9 us (0.958)
  Pallas kernels: 74.9 us -> 71.8 us
    pallas_call x1, Pallas kernels: 74.9 us -> 71.8 us  [per_device(): pl.pallas_call(music_kernel, out_shape=(pltpu.VMEM((BLOCK, 2 * BLOCK), F3...]
where the time goes in v4:
time: 73.9 us; the launch traced here: 73.7 us
  Pallas kernels  71.8 us (97%)
  local copies, waits for them, and re-layouts  1.27 us (2%)
    pallas_call x1, Pallas kernels, per_device(): pl.pallas_call(music_kernel, out_shape=(pltpu.VMEM((BLOCK, 2 * BLOCK), F3...  71.8 us

profile of v4, /device:TPU:1, one launch (start us, length us, event | category | flops | bytes accessed | tf_op | source)
XLA Modules:
  0.0 73.7 jit_solution(15265443640514689024)
XLA Ops:
  0.6 71.8 %music.1 = (f32[128,256]{1,0:T(8,128)S(1)}, f32[64,128]{1,0:T(8,128)S(1)}) custom-call(bf16[256,128]{1,0:T(8,128)(2,1)} %bitcast.2, bf16[256,128]{1,0:T(8,128)(2,1)} %bitcast.3, s32[3]{0:T(128)} %offs_ref.1, f32[64,128]{1,0:T(8,128)} %start_any.1), custom_call_target="tpu_custom_call" | custom-call | tf_op jit(solution)/shard_map/music/pallas_call | solution.py:455
  72.4 0.7 copy.8
  73.1 0.6 copy.9

commit v5 on v4

--- a/solution.py
+++ b/solution.py
@@ -80,6 +80,48 @@
     return jnp.concatenate(out, 0)[:, :64]
 
 
+def packed_places():
+    lanes = lax.broadcasted_iota(jnp.int32, (8, 128), 1)
+    subs = lax.broadcasted_iota(jnp.int32, (8, 128), 0)
+    group = sum(jnp.where(lanes >= 32 * g, 1, 0) for g in (1, 2, 3))
+    return lanes, subs + 8 * group, lanes - 32 * group
+
+
+def packed_gram(x):
+    lanes, row, column = packed_places()
+
+    def repeated(a, b):
+        return lax.dot_general(
+            a, jnp.concatenate([b] * 4, 0), (((1,), (1,)), ((), ())), precision=HIGHEST, preferred_element_type=F32
+        )
+
+    def packed(tiles):
+        out = tiles[24:32]
+        for g in (2, 1, 0):
+            out = jnp.where(lanes < 32 * (g + 1), tiles[8 * g : 8 * g + 8], out)
+        return out
+
+    first, second = repeated(x, x[:32]), repeated(x[32:], x[32:])
+    last = packed(second)
+    mixed = jnp.where(row >= column, packed(first[:32]), last)
+    return packed(first[32:]), mixed, jnp.sum(jnp.where(row == column, last, 0.0), axis=0, keepdims=True)
+
+
+def unpacked_gram(corner, mixed, diagonal):
+    lanes, row, column = packed_places()
+    same = row == column
+    upper = jnp.where(row > column, mixed, jnp.where(same, 0.5 * mixed, 0.0))
+    lower = jnp.where(row < column, mixed, jnp.where(same, 0.5 * diagonal, 0.0))
+    top, bottom = [], []
+    for g in range(4):
+        back = (128 - 32 * g) % 128
+        top.append(jnp.where(lanes < 32, pltpu.roll(upper, back, 1), 0.0))
+        left, right = pltpu.roll(corner, back, 1), pltpu.roll(lower, (back + 32) % 128, 1)
+        bottom.append(jnp.where(lanes < 32, left, jnp.where(lanes < 64, right, 0.0)))
+    half = jnp.concatenate(top + bottom, 0)[:, :K]
+    return jnp.concatenate([jnp.zeros((K, K), F32), half + half.T], 1)
+
+
 def padded_gram(x):
     both = jnp.concatenate([jnp.zeros_like(x), x], 0)
     return lax.dot_general(x, both, (((1,), (1,)), ((), ())), precision=HIGHEST, preferred_element_type=F32)
@@ -101,11 +143,11 @@
 
 
 def music_kernel(
-    own_any, tail_any, offs_ref, start_any, cov_ref, basis_ref,
+    own_any, tail_any, offs_ref, start_any, cov_ref, mapped_ref, gram_ref,
     own_ref, tail_ref, start_ref,
     got, picks, offs_all, offs_near, offs_now,
     row_w, row_m, col_w, col_m, acc,
-    part1, land1, map1, part2, land2, sum2, part3, land3, sum3,
+    part1, land1, map1, part2, land2, sum2, part3, land3, sum3, partd, landd,
     wide_send, wide_recv, pair_send, pair_recv, near_send, near_recv, offs_send, offs_recv, local_sem,
     send_sem, recv_sem,
 ):
@@ -233,33 +275,6 @@
         offs_copy(dest).start()
     offs_all[t] = offs_near[...]
 
-    for slot, block, source, column, opposite in slots:
-        @pl.when(opposite)
-        def _():
-            wide(slot, 0, r).wait_recv()
-            along_y(slot)
-
-    for slot in range(3):
-        def body():
-            near(slot, r).wait_recv()
-
-            for dest in places:
-                pass_on(slot, piece, dest).start()
-
-        when(gets_near[slot], body)
-
-    for slot, block, source, column, opposite in slots:
-        @pl.when(column)
-        def _():
-            wide(slot, 0, r).wait_recv()
-            along_x(slot)
-
-    for slot, block, source, column, opposite in slots:
-        if shared(slot):
-            waits = jnp.logical_not(source | column | opposite)
-            pl.when(waits)(lambda: wide(slot, 0, r).wait_recv())
-            pl.when(jnp.logical_not(source))(lambda: pair(slot, half).start())
-
     picks[0] = selection(r < ROWS // 2, False)
     picks[1] = selection(r < ROWS // 2, True)
     picks[2] = selection(t < COLS // 2, False)
@@ -290,10 +305,38 @@
 
     def put(window, pick, place, block):
         both = jnp.dot(picks[pick], block, preferred_element_type=F32) * HALF_ROOT
-        window[0, pl.ds(place * BLOCK, BLOCK), :] = both[:BLOCK]
-        window[1, pl.ds(place * BLOCK, BLOCK), :] = both[BLOCK:]
+        span = pl.ds(pl.multiple_of(place * BLOCK, BLOCK), BLOCK)
+        window[0, span, :] = both[:BLOCK]
+        window[1, span, :] = both[BLOCK:]
 
     put(row_w, 0, 0, own_ref[...])
+
+    for slot, block, source, column, opposite in slots:
+        @pl.when(opposite)
+        def _():
+            wide(slot, 0, r).wait_recv()
+            along_y(slot)
+
+    for slot in range(3):
+        def body():
+            near(slot, r).wait_recv()
+
+            for dest in places:
+                pass_on(slot, piece, dest).start()
+
+        when(gets_near[slot], body)
+
+    for slot, block, source, column, opposite in slots:
+        @pl.when(column)
+        def _():
+            wide(slot, 0, r).wait_recv()
+            along_x(slot)
+
+    for slot, block, source, column, opposite in slots:
+        if shared(slot):
+            waits = jnp.logical_not(source | column | opposite)
+            pl.when(waits)(lambda: wide(slot, 0, r).wait_recv())
+            pl.when(jnp.logical_not(source))(lambda: pair(slot, half).start())
 
     every_offs = offs_all.at[pl.ds(0, COLS - 1)]
     whole_offs = pltpu.make_async_remote_copy(
@@ -319,13 +362,15 @@
         if not shared(slot):
             waits = (block < ROWS) & jnp.logical_not(source | column | opposite)
             pl.when(waits)(lambda: wide(slot, 0, r).wait_recv())
+    put(col_w, 2, 1, got[4])
+    put(col_m, 3, 1, got[7])
+    put(col_w, 2, 2 * core, got[5])
+    put(col_m, 3, 2 * core, got[8])
     for slot, block, source, column, opposite in slots:
         if shared(slot):
             pl.when(jnp.logical_not(source))(lambda: pair(slot, other).wait_recv())
-    low, high = 2 - 2 * core, 2 * core
-    for place, (w, m) in enumerate(((3 + low, 6 + low), (4, 7), (3 + high, 6 + high))):
-        put(col_w, 2, place, got[w])
-        put(col_m, 3, place, got[m])
+    put(col_w, 2, 2 - 2 * core, got[3])
+    put(col_m, 3, 2 - 2 * core, got[6])
     to_scalar.wait()
 
     def pairs(window, mirror, offset, count):
@@ -402,22 +447,25 @@
     total(3, sum2, COLS - 1).wait_recv()
     factor1 = lower_inverse(sum2[8:16].reshape(K, BLOCK))
     mapped2 = jnp.dot(factor1, sum2[0:8].reshape(K, BLOCK), precision=HIGHEST, preferred_element_type=F32)
-    gram2 = padded_gram(mapped2)
-    for a in range(16):
-        part3[a] = gram2[4 * a : 4 * a + 4]
-
+    corner, mixed, diagonal = packed_gram(mapped2)
+    part3[...] = jnp.where(core == 0, corner, mixed)
+    partd[...] = diagonal
     for dest in rows:
-        copy(part3.at[t], land3.at[r], 4, {"row": dest}).start()
-    land3[r] = part3[t]
+        copy(part3, land3.at[r], 4, {"row": dest}).start()
+    for dest in rows:
+        copy(partd, landd.at[r], 6, {"row": dest}).start()
+    land3[r] = part3[...]
+    landd[r] = partd[...]
     total(4, land3, ROWS - 1).wait_recv()
-    sum3[t] = jnp.sum(land3[...], axis=0)
-
-    for dest in places:
-        copy(sum3.at[t], sum3.at[t], 5, {"shift": dest}).start()
-    total(5, sum3, COLS - 1).wait_recv()
-    whole = jnp.concatenate([sum3[a] for a in range(16)], 0)
-    factor2 = lower_inverse(whole)
-    basis_ref[...] = jnp.dot(factor2, mapped2, precision=HIGHEST, preferred_element_type=F32)
+    sum3[core] = jnp.sum(land3[...], axis=0)
+    halves = copy(sum3.at[core], sum3.at[core], 5, {"shift": t + 1 - 2 * core})
+    halves.start()
+    total(6, landd, ROWS - 1).wait_recv()
+    diagonal = jnp.broadcast_to(jnp.sum(landd[...], axis=0), (8, 128))
+    halves.wait_recv()
+    whole = unpacked_gram(sum3[0], sum3[1], diagonal)
+    mapped_ref[...] = mapped2
+    gram_ref[...] = whole
 
     for slot, block, source, column, opposite in slots:
         def drain(low, high):
@@ -441,7 +489,17 @@
     total(2, land2, COLS - 1).wait_send()
     total(3, sum2, COLS - 1).wait_send()
     total(4, land3, ROWS - 1).wait_send()
-    total(5, sum3, COLS - 1).wait_send()
+    halves.wait_send()
+    total(6, landd, ROWS - 1).wait_send()
+
+
+def finish_kernel(cov_ref, mapped_ref, gram_ref, cov_out, basis_ref, sem):
+    write = pltpu.make_async_copy(cov_ref, cov_out, sem)
+    write.start()
+    basis_ref[...] = jnp.dot(
+        lower_inverse(gram_ref[...]), mapped_ref[...], precision=HIGHEST, preferred_element_type=F32
+    )
+    write.wait()
 
 
 def per_device(snapshots, tail_sensors, shift_offsets, start_basis):
@@ -452,14 +510,15 @@
     hbm = pl.BlockSpec(memory_space=pl.ANY)
     dma = pltpu.SemaphoreType.DMA
     f32 = lambda *shape: pltpu.VMEM(shape, F32)
-    return pl.pallas_call(
+    cov, mapped, gram = pl.pallas_call(
         music_kernel,
         out_shape=(
             pltpu.VMEM((BLOCK, 2 * BLOCK), F32),
             pltpu.VMEM((K, BLOCK), F32),
+            pltpu.VMEM((K, BLOCK), F32),
         ),
         in_specs=[hbm, hbm, smem, hbm],
-        out_specs=(vmem, vmem),
+        out_specs=(vmem, vmem, vmem),
         scratch_shapes=[
             pltpu.VMEM((256, 128), BF16), pltpu.VMEM((256, 128), BF16), f32(K, BLOCK),
             pltpu.VMEM((9, 256, 128), BF16), pltpu.VMEM((4, 256, 256), BF16),
@@ -468,13 +527,24 @@
             f32(2, 256, 128), f32(2, 256, 128), f32(2, 384, 128), f32(2, 384, 128), f32(128, 256),
             f32(32, 4, 128), f32(32, 4, 128), f32(32, 4, 128),
             f32(16, 8, 128), f32(16, 8, 128), f32(16, 8, 128),
-            f32(16, 4, 128), f32(32, 4, 128), f32(16, 4, 128),
+            f32(8, 128), f32(32, 8, 128), f32(2, 8, 128), f32(1, 128), f32(32, 1, 128),
             dma((6, 10)), dma((6,)), dma((2,)), dma((2,)), dma((3, 2)), dma((3, 2)), dma, dma, dma((4,)),
-            dma((6,)), dma((6,)),
+            dma((7,)), dma((7,)),
         ],
         compiler_params=pltpu.CompilerParams(collective_id=0, has_side_effects=True),
         name="music",
     )(own, tail, shift_offsets, start_basis)
+    return pl.pallas_call(
+        finish_kernel,
+        out_shape=(
+            jax.ShapeDtypeStruct((BLOCK, 2 * BLOCK), F32),
+            jax.ShapeDtypeStruct((K, BLOCK), F32),
+        ),
+        in_specs=[vmem, vmem, vmem],
+        out_specs=(hbm, vmem),
+        scratch_shapes=[dma],
+        name="finish",
+    )(*(pltpu.with_memory_space_constraint(x, pltpu.VMEM) for x in (cov, mapped, gram)))
 
 
 def solution(mesh):

time: 73.9 us -> 71.6 us (0.969)
  local copies, waits for them, and re-layouts: 1.27 us -> 0 us
  Pallas kernels: 71.8 us -> 70.7 us
    pallas_call x1, Pallas kernels: 71.8 us -> 68.5 us  [per_device(): pl.pallas_call(music_kernel, out_shape=(pltpu.VMEM((BLOCK, 2 * BLOCK), F3...]
    pallas_call x0 -> x1, Pallas kernels: none -> 2.27 us  [per_device(): pl.pallas_call(finish_kernel, out_shape=(jax.ShapeDtypeStruct((BLOCK, 2 *...]
    unnamed x2 -> x0, local copies, waits for them, and re-layouts: 1.27 us -> none
where the time goes in v5:
time: 71.6 us; the launch traced here: 71.4 us
  Pallas kernels  70.7 us (99%)
    pallas_call x1, Pallas kernels, per_device(): pl.pallas_call(music_kernel, out_shape=(pltpu.VMEM((BLOCK, 2 * BLOCK), F3...  68.5 us
    pallas_call x1, Pallas kernels, per_device(): pl.pallas_call(finish_kernel, out_shape=(jax.ShapeDtypeStruct((BLOCK, 2 *...  2.27 us

profile of v5, /device:TPU:1, one launch (start us, length us, event | category | flops | bytes accessed | tf_op | source)
XLA Modules:
  0.0 71.4 jit_solution(11710299618954832451)
XLA Ops:
  0.6 68.5 %music.1 = (f32[128,256]{1,0:T(8,128)S(1)}, f32[64,128]{1,0:T(8,128)S(1)}, f32[64,128]{1,0:T(8,128)S(1)}) custom-call(bf16[256,128]{1,0:T(8,128)(2,1)} %bitcast.2, bf16[256,128]{1,0:T(8,128)(2,1)} %bitcast.3, s32[3]{0:T(128)} %offs_ref.1, f32[64,128]{1,0:T(8,128)} %start_any.1), custom_call_target="tpu_custom_call" | custom-call | tf_op jit(solution)/shard_map/music/pallas_call | solution.py:513
  69.1 2.3 %finish.1 = (f32[128,256]{1,0:T(8,128)}, f32[64,128]{1,0:T(8,128)}) custom-call(f32[128,256]{1,0:T(8,128)S(1)} %get-tuple-element.5.cov_ref, f32[64,128]{1,0:T(8,128)S(1)} %get-tuple-element.6.mapped_ref, f32[64,128]{1,0:T(8,128)S(1)} %get-tuple-element.7.gram_ref), custom_call_target="tpu_custom_call" | custom-call | tf_op jit(solution)/shard_map/finish/pallas_call | solution.py:537

commit v6 on v5

--- a/solution.py
+++ b/solution.py
@@ -122,11 +122,6 @@
     return jnp.concatenate([jnp.zeros((K, K), F32), half + half.T], 1)
 
 
-def padded_gram(x):
-    both = jnp.concatenate([jnp.zeros_like(x), x], 0)
-    return lax.dot_general(x, both, (((1,), (1,)), ((), ())), precision=HIGHEST, preferred_element_type=F32)
-
-
 def selection(top, flipped):
     out = lax.broadcasted_iota(jnp.int32, (2 * BLOCK, 2 * BLOCK), 0)
     src = lax.broadcasted_iota(jnp.int32, (2 * BLOCK, 2 * BLOCK), 1)
@@ -147,7 +142,7 @@
     own_ref, tail_ref, start_ref,
     got, picks, offs_all, offs_near, offs_now,
     row_w, row_m, col_w, col_m, acc,
-    part1, land1, map1, part2, land2, sum2, part3, land3, sum3, partd, landd,
+    part1, land1, map1, part2, beside, middle, land2, sum2, part3, land3, sum3, partd, landd,
     wide_send, wide_recv, pair_send, pair_recv, near_send, near_recv, offs_send, offs_recv, local_sem,
     send_sem, recv_sem,
 ):
@@ -428,25 +423,42 @@
         [jnp.concatenate([map1[16 * c + a] for a in range(16)], 0) for c in range(2)], 1
     )
 
-    gram1 = padded_gram(mapped)
+    lanes = lax.broadcasted_iota(jnp.int32, (8, BLOCK), 1)
+    gram1 = lax.dot_general(
+        mapped, jnp.concatenate([mapped, mapped], 0), (((1,), (1,)), ((), ())), precision=HIGHEST, preferred_element_type=F32
+    )
     second = lax.dot_general(
         mapped, cov_ref[...], (((1,), (1,)), ((), ())), precision=HIGHEST, preferred_element_type=F32
     )
-    for a in range(8):
-        part2[a] = second[8 * a : 8 * a + 8]
-        part2[8 + a] = gram1[8 * a : 8 * a + 8]
-
-    for dest in places:
-        copy(part2.at[dest], land2.at[t], 2, {"shift": dest}).start()
-    land2[t] = part2[t]
-    total(2, land2, COLS - 1).wait_recv()
-    sum2[t] = jnp.sum(land2[...], axis=0)
-
-    for dest in places:
-        copy(sum2.at[t], sum2.at[t], 3, {"shift": dest}).start()
-    total(3, sum2, COLS - 1).wait_recv()
-    factor1 = lower_inverse(sum2[8:16].reshape(K, BLOCK))
-    mapped2 = jnp.dot(factor1, sum2[0:8].reshape(K, BLOCK), precision=HIGHEST, preferred_element_type=F32)
+    for h in range(2):
+        for i in range(4):
+            part2[h, i] = second[32 * h + 8 * i : 32 * h + 8 * i + 8]
+        for i in range(2):
+            a = 16 * h + 8 * i
+            part2[h, 4 + i] = jnp.where(lanes < K, gram1[a : a + 8], gram1[32 + a : 40 + a])
+    partner = {"shift": t + 1 - 2 * core}
+    meet = copy(part2.at[1 - core], beside, 2, partner)
+    meet.start()
+    meet.wait_recv()
+    middle[...] = part2[core] + beside[...]
+    for b in far_first(8):
+        if b:
+            copy(middle, land2.at[z], 3, {"shift": lax.rem(z + b, 8) * 2 + core}).start()
+    land2[z] = middle[...]
+    total(3, land2, 7).wait_recv()
+    sum2[core] = jnp.sum(land2[...], axis=0)
+    swap = copy(sum2.at[core], sum2.at[core], 7, partner)
+    swap.start()
+    swap.wait_recv()
+    tiles = [sum2[h, 4 + i] for h in range(2) for i in range(2)]
+    gram1 = jnp.concatenate(
+        [jnp.where(lanes < K, 0.0, pltpu.roll(tile, K, 1)) for tile in tiles]
+        + [jnp.where(lanes < K, 0.0, tile) for tile in tiles],
+        0,
+    )
+    factor1 = lower_inverse(gram1)
+    product = jnp.concatenate([sum2[h, i] for h in range(2) for i in range(4)], 0)
+    mapped2 = jnp.dot(factor1, product, precision=HIGHEST, preferred_element_type=F32)
     corner, mixed, diagonal = packed_gram(mapped2)
     part3[...] = jnp.where(core == 0, corner, mixed)
     partd[...] = diagonal
@@ -486,8 +498,9 @@
     whole_offs.wait_send()
     total(0, land1, ROWS - 1).wait_send()
     total(1, map1, ROWS - 1).wait_send()
-    total(2, land2, COLS - 1).wait_send()
-    total(3, sum2, COLS - 1).wait_send()
+    meet.wait_send()
+    total(3, land2, 7).wait_send()
+    swap.wait_send()
     total(4, land3, ROWS - 1).wait_send()
     halves.wait_send()
     total(6, landd, ROWS - 1).wait_send()
@@ -526,10 +539,10 @@
             pltpu.SMEM((COLS, 1, BLOCK), jnp.int32),
             f32(2, 256, 128), f32(2, 256, 128), f32(2, 384, 128), f32(2, 384, 128), f32(128, 256),
             f32(32, 4, 128), f32(32, 4, 128), f32(32, 4, 128),
-            f32(16, 8, 128), f32(16, 8, 128), f32(16, 8, 128),
+            f32(2, 6, 8, 128), f32(6, 8, 128), f32(6, 8, 128), f32(8, 6, 8, 128), f32(2, 6, 8, 128),
             f32(8, 128), f32(32, 8, 128), f32(2, 8, 128), f32(1, 128), f32(32, 1, 128),
             dma((6, 10)), dma((6,)), dma((2,)), dma((2,)), dma((3, 2)), dma((3, 2)), dma, dma, dma((4,)),
-            dma((7,)), dma((7,)),
+            dma((8,)), dma((8,)),
         ],
         compiler_params=pltpu.CompilerParams(collective_id=0, has_side_effects=True),
         name="music",

time: 71.6 us -> 70.7 us (0.987)
  Pallas kernels: 70.7 us -> 69.9 us
    pallas_call x1, Pallas kernels: 68.5 us -> 67.6 us  [per_device(): pl.pallas_call(music_kernel, out_shape=(pltpu.VMEM((BLOCK, 2 * BLOCK), F3...]
where the time goes in v6:
time: 70.7 us; the launch traced here: 70.5 us
  Pallas kernels  69.9 us (99%)
    pallas_call x1, Pallas kernels, per_device(): pl.pallas_call(music_kernel, out_shape=(pltpu.VMEM((BLOCK, 2 * BLOCK), F3...  67.6 us
    pallas_call x1, Pallas kernels, per_device(): pl.pallas_call(finish_kernel, out_shape=(jax.ShapeDtypeStruct((BLOCK, 2 *...  2.27 us

profile of v6, /device:TPU:1, one launch (start us, length us, event | category | flops | bytes accessed | tf_op | source)
XLA Modules:
  0.0 70.5 jit_solution(15701393117950318781)
XLA Ops:
  0.6 67.6 %music.1 = (f32[128,256]{1,0:T(8,128)S(1)}, f32[64,128]{1,0:T(8,128)S(1)}, f32[64,128]{1,0:T(8,128)S(1)}) custom-call(bf16[256,128]{1,0:T(8,128)(2,1)} %bitcast.2, bf16[256,128]{1,0:T(8,128)(2,1)} %bitcast.3, s32[3]{0:T(128)} %offs_ref.1, f32[64,128]{1,0:T(8,128)} %start_any.1), custom_call_target="tpu_custom_call" | custom-call | tf_op jit(solution)/shard_map/music/pallas_call | solution.py:526
  68.2 2.3 %finish.1 = (f32[128,256]{1,0:T(8,128)}, f32[64,128]{1,0:T(8,128)}) custom-call(f32[128,256]{1,0:T(8,128)S(1)} %get-tuple-element.5.cov_ref, f32[64,128]{1,0:T(8,128)S(1)} %get-tuple-element.6.mapped_ref, f32[64,128]{1,0:T(8,128)S(1)} %get-tuple-element.7.gram_ref), custom_call_target="tpu_custom_call" | custom-call | tf_op jit(solution)/shard_map/finish/pallas_call | solution.py:550

commit v7 on v6

--- a/solution.py
+++ b/solution.py
@@ -144,18 +144,28 @@
     row_w, row_m, col_w, col_m, acc,
     part1, land1, map1, part2, beside, middle, land2, sum2, part3, land3, sum3, partd, landd,
     wide_send, wide_recv, pair_send, pair_recv, near_send, near_recv, offs_send, offs_recv, local_sem,
-    send_sem, recv_sem,
+    send_sem, recv_sem, ready,
 ):
     r = lax.axis_index("row")
     t = lax.axis_index("shift")
     x, y = lax.div(r, 8), lax.rem(r, 8)
     z, core = lax.div(t, 2), lax.rem(t, 2)
     rows, places = plane_peers(r), line_peers(t)
-    column_rows = [x * 8 + lax.rem(y + b, 8) for b in far_first(8) if b]
+    column_rows = [x * 8 + lax.rem(y + b, 8) for b in (3, 5, 4, 2, 6, 1, 7)]
     bring_own = pltpu.make_async_copy(own_any, own_ref, local_sem.at[1])
     bring_own.start()
     barrier = pltpu.get_barrier_semaphore()
-    signal_peers(barrier, rows, places)
+    across_rows = [lax.rem(x + d, 4) * 8 + y for d in (2, 1, 3)]
+    signal_peers(barrier, column_rows + across_rows + [31 - r], places)
+
+    @pl.when(r < ROWS - 1)
+    def _():
+        signal_peers(barrier, [r + 1], [])
+
+    @pl.when((r >= 1) & (r != ROWS // 2))
+    def _():
+        signal_peers(barrier, [32 - r], [])
+
     bring_tail = pltpu.make_async_copy(tail_any, tail_ref, local_sem.at[2])
     bring_tail.start()
     bring_start = pltpu.make_async_copy(start_any, start_ref, local_sem.at[3])
@@ -167,7 +177,9 @@
     other = pl.ds(pl.multiple_of((1 - core) * BLOCK, BLOCK), BLOCK)
     piece = pl.ds(pl.multiple_of(t * 16, 16), 16)
     bring_own.wait()
-    pl.semaphore_wait(barrier, ROWS - 1 + COLS - 1)
+    extra = jnp.where(r >= 1, 1, 0) + jnp.where((r >= 1) & (r != ROWS // 2), 1, 0)
+    pl.semaphore_wait(barrier, 11 + COLS - 1 + extra)
+    signal_peers(ready, across_rows, [])
 
     slots = []
     for group in range(2):
@@ -321,7 +333,7 @@
 
         when(gets_near[slot], body)
 
-    for slot, block, source, column, opposite in slots:
+    for slot, block, source, column, opposite in [slots[i] for i in (1, 4, 0, 3, 2, 5)]:
         @pl.when(column)
         def _():
             wide(slot, 0, r).wait_recv()
@@ -410,6 +422,7 @@
         every = buffer.at[pl.ds(0, count)]
         return copy(every, every, phase, {"row": r})
 
+    pl.semaphore_wait(ready, 3)
     for dest in rows:
         copy(part1.at[dest], land1.at[r], 0, {"row": dest}).start()
     land1[r] = part1[r]
@@ -542,7 +555,7 @@
             f32(2, 6, 8, 128), f32(6, 8, 128), f32(6, 8, 128), f32(8, 6, 8, 128), f32(2, 6, 8, 128),
             f32(8, 128), f32(32, 8, 128), f32(2, 8, 128), f32(1, 128), f32(32, 1, 128),
             dma((6, 10)), dma((6,)), dma((2,)), dma((2,)), dma((3, 2)), dma((3, 2)), dma, dma, dma((4,)),
-            dma((8,)), dma((8,)),
+            dma((8,)), dma((8,)), pltpu.SemaphoreType.REGULAR,
         ],
         compiler_params=pltpu.CompilerParams(collective_id=0, has_side_effects=True),
         name="music",

time: 70.7 us -> 70.3 us (level)
  no operation moved by 1% of the time
where the time goes in v7:
time: 70.3 us; the launch traced here: 70.1 us
  Pallas kernels  69.5 us (99%)
    pallas_call x1, Pallas kernels, per_device(): pl.pallas_call(music_kernel, out_shape=(pltpu.VMEM((BLOCK, 2 * BLOCK), F3...  67.2 us
    pallas_call x1, Pallas kernels, per_device(): pl.pallas_call(finish_kernel, out_shape=(jax.ShapeDtypeStruct((BLOCK, 2 *...  2.27 us

profile of v7, /device:TPU:1, one launch (start us, length us, event | category | flops | bytes accessed | tf_op | source)
XLA Modules:
  0.0 70.1 jit_solution(8156298288489666594)
XLA Ops:
  0.6 67.2 %music.1 = (f32[128,256]{1,0:T(8,128)S(1)}, f32[64,128]{1,0:T(8,128)S(1)}, f32[64,128]{1,0:T(8,128)S(1)}) custom-call(bf16[256,128]{1,0:T(8,128)(2,1)} %bitcast.2, bf16[256,128]{1,0:T(8,128)(2,1)} %bitcast.3, s32[3]{0:T(128)} %offs_ref.1, f32[64,128]{1,0:T(8,128)} %start_any.1), custom_call_target="tpu_custom_call" | custom-call | tf_op jit(solution)/shard_map/music/pallas_call | solution.py:539
  67.8 2.3 %finish.1 = (f32[128,256]{1,0:T(8,128)}, f32[64,128]{1,0:T(8,128)}) custom-call(f32[128,256]{1,0:T(8,128)S(1)} %get-tuple-element.5.cov_ref, f32[64,128]{1,0:T(8,128)S(1)} %get-tuple-element.6.mapped_ref, f32[64,128]{1,0:T(8,128)S(1)} %get-tuple-element.7.gram_ref), custom_call_target="tpu_custom_call" | custom-call | tf_op jit(solution)/shard_map/finish/pallas_call | solution.py:563

commit v8 on v7

--- a/solution.py
+++ b/solution.py
@@ -390,8 +390,8 @@
 
     def some(i, c):
         lhs, rhs = [], []
-        for j in range(12):
-            offset = offs_now[i * 4 + j // 3, 0, j % 3]
+        for j in range(24):
+            offset = offs_now[i * 8 + j // 3, 0, j % 3]
             lhs += pairs(row_w, row_m, offset, BLOCK)
             rhs += pairs(col_w, col_m, offset, 2 * BLOCK)
         acc[...] += lax.dot_general(
@@ -399,7 +399,7 @@
         )
         return c
 
-    lax.fori_loop(0, 4, some, 0)
+    lax.fori_loop(0, 2, some, 0)
     cov = acc[...] * (1.0 / (SNAPS * SHIFTS))
     cov_ref[...] = cov
 

time: 70.3 us -> 70 us (level)
  no operation moved by 1% of the time
where the time goes in v8:
time: 70 us; the launch traced here: 69.8 us
  Pallas kernels  69.2 us (99%)
    pallas_call x1, Pallas kernels, per_device(): pl.pallas_call(music_kernel, out_shape=(pltpu.VMEM((BLOCK, 2 * BLOCK), F3...  66.9 us
    pallas_call x1, Pallas kernels, per_device(): pl.pallas_call(finish_kernel, out_shape=(jax.ShapeDtypeStruct((BLOCK, 2 *...  2.27 us

profile of v8, /device:TPU:1, one launch (start us, length us, event | category | flops | bytes accessed | tf_op | source)
XLA Modules:
  0.0 69.8 jit_solution(11289413398190993853)
XLA Ops:
  0.6 66.9 %music.1 = (f32[128,256]{1,0:T(8,128)S(1)}, f32[64,128]{1,0:T(8,128)S(1)}, f32[64,128]{1,0:T(8,128)S(1)}) custom-call(bf16[256,128]{1,0:T(8,128)(2,1)} %bitcast.2, bf16[256,128]{1,0:T(8,128)(2,1)} %bitcast.3, s32[3]{0:T(128)} %offs_ref.1, f32[64,128]{1,0:T(8,128)} %start_any.1), custom_call_target="tpu_custom_call" | custom-call | tf_op jit(solution)/shard_map/music/pallas_call | solution.py:539
  67.5 2.3 %finish.1 = (f32[128,256]{1,0:T(8,128)}, f32[64,128]{1,0:T(8,128)}) custom-call(f32[128,256]{1,0:T(8,128)S(1)} %get-tuple-element.5.cov_ref, f32[64,128]{1,0:T(8,128)S(1)} %get-tuple-element.6.mapped_ref, f32[64,128]{1,0:T(8,128)S(1)} %get-tuple-element.7.gram_ref), custom_call_target="tpu_custom_call" | custom-call | tf_op jit(solution)/shard_map/finish/pallas_call | solution.py:563
